TPU v7x, 256 devices: a whole 4x4x8 slice. The times are simulated.
256 devices in a mesh: ta: 64 (over y, z_hi, x, core), ga: 4 (over z_lo).
Axes of the slice: x: 4, y: 4, z: 8 (z_hi: 2, z_lo: 4; z = z_hi * 4 + z_lo), core: 2. Of those that a mesh axis runs over, the one named last changes fastest.
Arguments:
- snapshots: bfloat16 [1024, 4, 131072], P('ta', 'ga'), may hold values from -12 to 12
- block_starts: int32 [7], replicated, may hold values from 0 to 768
- kept_freqs: int32 [32], replicated, may hold values from 0 to 128
Outputs:
- spectra: bfloat16 [4, 7, 2, 32, 131072], P('ga', None, None, None, 'ta')
- power_step: float32 [4, 7, 2, 32, 131072], P('ga', None, None, None, 'ta')
All inputs are finite; a program needn't handle non-finite values.
Results may differ from a plain program's by a relative error of at most 0.0047.
Values may be sent and summed in bfloat16 or wider, within the bound.
No kernel may reach another device: no remote copies, remote signals or barrier semaphores. Data moves between devices by JAX's collectives and lax.ppermute only.
A program may use at most 192 MiB of HBM per device.

v0:
```python
import functools
import math

import jax
import jax.numpy as jnp
from jax import lax
from jax.experimental import pallas as pl
from jax.experimental.pallas import tpu as pltpu
from jax.sharding import Mesh
from jax.sharding import PartitionSpec as P


NFFT = 256
NB = 7
NF = 32
HALF = NB * NF
ROWS = 2 * HALF
PAIRS = NB // 2
TA = ("y", "zh", "x", "c")
PLANE = ("y", "x", "c")
FIRST = 640
LAST = 512
F32 = jnp.float32
BF16 = jnp.bfloat16


def weights(block_starts, kept_freqs, times):
    offset = times[None, :] - block_starts[:, None]
    inside = (offset >= 0) & (offset < NFFT)
    window = 0.5 - 0.5 * jnp.cos(2.0 * math.pi / NFFT * offset.astype(F32))
    scale = jnp.where(inside, window, 0.0)
    phase = kept_freqs[None, :, None] * jnp.where(inside, offset, 0)[:, None, :] % NFFT
    angle = 2.0 * math.pi / NFFT * phase.astype(F32)
    norm = 2.0 / math.sqrt(NFFT)
    real = scale[:, None, :] * jnp.cos(angle) * norm
    imag = -scale[:, None, :] * jnp.sin(angle) * norm
    table = jnp.stack([real, imag]).astype(BF16)
    return table.reshape(ROWS, times.shape[0])


def dot(a, b):
    return jnp.dot(a, b, preferred_element_type=F32)


def dot_t(a, b):
    return lax.dot_general(a, b, (((1,), (1,)), ((), ())), preferred_element_type=F32)


def same_freq(rows):
    row = lax.broadcasted_iota(jnp.int32, (rows, HALF), 0)
    col = lax.broadcasted_iota(jnp.int32, (rows, HALF), 1)
    return row % NF == col % NF


def pack_kernel(own, jobs, x_ref, *refs):
    outs, sems = refs[:-1], refs[-1]
    me = lax.axis_index("zh")
    copies = []
    for out, (shift, low) in zip(outs, jobs):
        side = (me + shift) % 2
        for d in range(out.shape[0]):
            start = ((d // 8) * 16 + d % 8) * own + low + side * (8 * own)
            cols = pl.ds(pl.multiple_of(start, 128), out.shape[2])
            copies.append(pltpu.make_async_copy(x_ref.at[:, cols], out.at[d], sems.at[len(copies)]))
    for copy in copies:
        copy.start()
    for copy in copies:
        copy.wait()


def pack(x, own, jobs):
    count = x.shape[1] // own // 2
    shapes = [jax.ShapeDtypeStruct((count, x.shape[0], n), x.dtype) for _, _, n in jobs]
    return pl.pallas_call(
        functools.partial(pack_kernel, own, [job[:2] for job in jobs]),
        out_shape=shapes,
        in_specs=[pl.BlockSpec(memory_space=pltpu.HBM)],
        out_specs=[pl.BlockSpec(memory_space=pltpu.VMEM)] * len(jobs),
        scratch_shapes=[pltpu.SemaphoreType.DMA((count * len(jobs),))],
        compiler_params=pltpu.CompilerParams(vmem_limit_bytes=60 * 2**20),
        name="pack",
    )(x)


def emit(parts, s_ref):
    for part in range(2):
        for b in range(NB):
            start = part * HALF + b * NF
            s_ref[b * 2 * NF + part * NF : b * 2 * NF + (part + 1) * NF, :] = parts[start : start + NF]


def gram_of(parts):
    real, imag = parts[:HALF], parts[HALF:]
    return jnp.concatenate([dot_t(real, real) + dot_t(imag, imag), dot_t(imag, real)], axis=0)


def rows_of(ref):
    return ref[...].reshape(-1, ref.shape[2])


def whole_kernel(w0_ref, w1_ref, x0_ref, x1_ref, g_ref, _, s_ref, out_ref, part_ref, sem):
    count = x1_ref.shape[2]
    low = x0_ref.shape[2] - count
    near = x0_ref[:, :, low:].reshape(-1, count)
    parts = (dot(w0_ref[...], near) + dot(w1_ref[...], rows_of(x1_ref))).astype(BF16)
    emit(parts, part_ref)
    save = pltpu.make_async_copy(part_ref, s_ref.at[:, pl.ds(low, count)], sem)
    save.start()
    out_ref[...] = g_ref[...] + gram_of(parts)
    save.wait()


def whole(w0, w1, x0, x1, g, s):
    times = w0.shape[1]
    count = x1.shape[2]
    here = pl.BlockSpec(memory_space=pltpu.VMEM)
    there = pl.BlockSpec(memory_space=pl.ANY)
    return pl.pallas_call(
        whole_kernel,
        out_shape=(
            jax.ShapeDtypeStruct(s.shape, BF16),
            jax.ShapeDtypeStruct((ROWS, HALF), F32),
            jax.ShapeDtypeStruct((ROWS, count), BF16),
        ),
        in_specs=[here] * 5 + [there],
        out_specs=(there, here, here),
        scratch_shapes=[pltpu.SemaphoreType.DMA],
        input_output_aliases={5: 0},
        compiler_params=pltpu.CompilerParams(vmem_limit_bytes=16 * 2**20),
        cost_estimate=pl.CostEstimate(flops=4 * ROWS * times * count, bytes_accessed=2**22, transcendentals=0),
        name="whole",
    )(w0, w1, x0, x1, g, s)


def partial_kernel(w_ref, x_ref, *p_refs):
    low = 0
    for p_ref in p_refs:
        count = p_ref.shape[1]
        p_ref[...] = dot(w_ref[...], x_ref[:, :, low : low + count].reshape(-1, count))
        low += count


def partial(w, x, counts):
    times = w.shape[1]
    here = pl.BlockSpec(memory_space=pltpu.VMEM)
    return pl.pallas_call(
        partial_kernel,
        out_shape=[jax.ShapeDtypeStruct((ROWS, count), F32) for count in counts],
        in_specs=[here, here],
        out_specs=[here] * len(counts),
        compiler_params=pltpu.CompilerParams(vmem_limit_bytes=16 * 2**20),
        cost_estimate=pl.CostEstimate(flops=2 * ROWS * times * sum(counts), bytes_accessed=2**21, transcendentals=0),
        name="partial",
    )(w, x)


def lane_block(rows):
    return lax.broadcasted_iota(jnp.int32, (rows, HALF), 1) // NF


def turned(row, k):
    lane = lax.broadcasted_iota(jnp.int32, row.shape, 1)
    near = pltpu.roll(row, 256 - k * NF, 1)
    far = pltpu.roll(row, HALF - k * NF, 1)
    return jnp.where(lane < HALF - k * NF, near, far)


def middle_kernel(w_ref, x_ref, p_ref, s_ref, out_ref, part_ref, sem):
    parts = (p_ref[...] + dot(w_ref[...], rows_of(x_ref))).astype(BF16)
    emit(parts, part_ref)
    save = pltpu.make_async_copy(part_ref, s_ref.at[:, pl.ds(0, parts.shape[1])], sem)
    save.start()
    out_ref[...] = gram_of(parts)
    save.wait()


def middle(w, x, p, pts):
    times = w.shape[1]
    width = x.shape[2]
    here = pl.BlockSpec(memory_space=pltpu.VMEM)
    return pl.pallas_call(
        middle_kernel,
        out_shape=(
            jax.ShapeDtypeStruct((ROWS, pts), BF16),
            jax.ShapeDtypeStruct((ROWS, HALF), F32),
            jax.ShapeDtypeStruct((ROWS, width), BF16),
        ),
        in_specs=[here] * 3,
        out_specs=(pl.BlockSpec(memory_space=pl.ANY), here, here),
        scratch_shapes=[pltpu.SemaphoreType.DMA],
        compiler_params=pltpu.CompilerParams(vmem_limit_bytes=16 * 2**20),
        cost_estimate=pl.CostEstimate(flops=2 * ROWS * times * width, bytes_accessed=2**22, transcendentals=0),
        name="middle",
    )(w, x, p)


def rest_kernel(low, w_ref, x_ref, p_ref, g_ref, _, s_ref, t_ref, part_ref, row_ref, sem):
    width = x_ref.shape[2]
    parts = (p_ref[...] + dot(w_ref[...], rows_of(x_ref))).astype(BF16)
    emit(parts, part_ref)
    save = pltpu.make_async_copy(part_ref, s_ref.at[:, pl.ds(low, width)], sem)
    save.start()
    kept = jnp.where(same_freq(ROWS), g_ref[...] + gram_of(parts), 0.0)
    tables = kept.reshape(2 * NB, NF, HALF).sum(axis=1)
    block = lax.broadcasted_iota(jnp.int32, (NB, HALF), 0)
    row_ref[...] = jnp.zeros_like(row_ref)
    for k in range(NB):
        pick = (lane_block(NB) + k) % NB == block
        if k <= PAIRS:
            row_ref[k : k + 1, :HALF] = jnp.where(pick, tables[:NB], 0.0).sum(axis=0, keepdims=True)
        if k:
            row_ref[NB + k : NB + k + 1, :HALF] = jnp.where(pick, tables[NB:], 0.0).sum(axis=0, keepdims=True)
    rows = [row_ref[k : k + 1, :] for k in range(2 * NB)]
    imag = [rows[NB + k] - turned(rows[2 * NB - k], k) for k in range(1, PAIRS + 1)]
    sums = jnp.concatenate(rows[: PAIRS + 1] + imag + [jnp.zeros_like(imag[0])], axis=0)
    for i in range(t_ref.shape[0]):
        t_ref[i] = sums
    save.wait()


def rest(w, x, p, g, s, low, copies):
    times = w.shape[1]
    width = x.shape[2]
    here = pl.BlockSpec(memory_space=pltpu.VMEM)
    there = pl.BlockSpec(memory_space=pl.ANY)
    return pl.pallas_call(
        functools.partial(rest_kernel, low),
        out_shape=(
            jax.ShapeDtypeStruct(s.shape, BF16),
            jax.ShapeDtypeStruct((copies, 8, 256), F32),
            jax.ShapeDtypeStruct((ROWS, width), BF16),
        ),
        in_specs=[here, here, here, here, there],
        out_specs=(there, here, here),
        scratch_shapes=[pltpu.VMEM((16, 256), F32), pltpu.SemaphoreType.DMA],
        input_output_aliases={4: 0},
        compiler_params=pltpu.CompilerParams(vmem_limit_bytes=16 * 2**20),
        cost_estimate=pl.CostEstimate(flops=2 * ROWS * times * width, bytes_accessed=2**22, transcendentals=0),
        name="rest",
    )(w, x, p, g, s)


def spread_to(part):
    row = lax.broadcasted_iota(jnp.int32, (HALF, ROWS), 0)
    col = lax.broadcasted_iota(jnp.int32, (HALF, ROWS), 1)
    return (col == row // NF * 2 * NF + part * NF + row % NF).astype(BF16)


def power_kernel(denominator, t_ref, *refs):
    part_refs, (o_ref, m_ref, out_ref, sem) = refs[:-4], refs[-4:]
    sums = jnp.sum(t_ref[...], axis=0) / denominator
    real_rows = [sums[k : k + 1, :] for k in range(PAIRS + 1)]
    imag_rows = [jnp.zeros_like(real_rows[0])] + [sums[PAIRS + k : PAIRS + k + 1, :] for k in range(1, PAIRS + 1)]
    for k in range(PAIRS + 1, NB):
        real_rows.append(turned(real_rows[NB - k], k))
        imag_rows.append(-turned(imag_rows[NB - k], k))
    block = lane_block(1)
    tables = []
    for rows in (real_rows, imag_rows):
        picked = [sum(jnp.where((block + k) % NB == b, rows[k][:, :HALF], 0.0) for k in range(NB)) for b in range(NB)]
        tables.append(jnp.concatenate(picked, axis=0).astype(BF16))
    real, imag = tables
    spread = [spread_to(part) for part in range(2)]
    from_real = dot(real, spread[0]) - dot(imag, spread[1])
    from_imag = dot(imag, spread[0]) + dot(real, spread[1])
    same = lax.broadcasted_iota(jnp.int32, (NF, ROWS), 0) == lax.broadcasted_iota(jnp.int32, (NF, ROWS), 1) % NF
    for b in range(NB):
        for part, table in enumerate((from_real, from_imag)):
            at = (2 * b + part) * NF
            row = jnp.broadcast_to(table[b : b + 1], (NF, ROWS))
            m_ref[at : at + NF, :] = jnp.where(same, row, 0.0).astype(BF16)
    stores = []
    low = 0
    for part_ref in part_refs:
        for at in range(0, part_ref.shape[1], 512):
            values = part_ref[:, at : at + 512]
            cols = pl.ds(low, values.shape[1])
            out_ref[:, low : low + values.shape[1]] = dot(m_ref[...], values)
            stores.append(pltpu.make_async_copy(out_ref.at[:, cols], o_ref.at[:, cols], sem.at[len(stores)]))
            stores[-1].start()
            low += values.shape[1]
    for store in stores:
        store.wait()


def power(t, parts, denominator):
    pts = sum(part.shape[1] for part in parts)
    here = pl.BlockSpec(memory_space=pltpu.VMEM)
    return pl.pallas_call(
        functools.partial(power_kernel, denominator),
        out_shape=jax.ShapeDtypeStruct((ROWS, pts), F32),
        in_specs=[here] * (1 + len(parts)),
        out_specs=pl.BlockSpec(memory_space=pl.ANY),
        scratch_shapes=[
            pltpu.VMEM((ROWS, ROWS), BF16),
            pltpu.VMEM((ROWS, pts), F32),
            pltpu.SemaphoreType.DMA((8,)),
        ],
        compiler_params=pltpu.CompilerParams(vmem_limit_bytes=16 * 2**20),
        name="power",
    )(t, *parts)


def to_all(t, axes):
    copies = jnp.broadcast_to(t[None], (lax.axis_size(axes), *t.shape))
    return lax.all_to_all(copies, axes, 0, 0, tiled=True)


def exchange(x, axes):
    return lax.all_to_all(x, axes, 0, 0, tiled=True)


def shards(snapshots, block_starts, kept_freqs):
    count = lax.axis_size(TA)
    local = snapshots.shape[0]
    own = snapshots.shape[2] // count
    total = own * count * lax.axis_size("zl")
    swap = [(0, 1), (1, 0)]
    x = snapshots.reshape(local, own * count)

    later = own - FIRST
    low = later - LAST
    (first,) = pack(x, own, [(1, later, FIRST)])
    first = lax.ppermute(first, "zh", swap)
    (pass_on,) = pack(x, own, [(1, 0, later)])
    pass_on = exchange(pass_on, PLANE)
    passed = lax.ppermute(pass_on[:, :, :low], "zh", swap)
    last = lax.ppermute(pass_on[:, :, low:], "zh", swap)
    (mine,) = pack(x, own, [(0, 0, own)])
    x0 = exchange(mine, PLANE)
    side = lax.axis_index("zh")
    place = jnp.arange(local * count // 2, dtype=jnp.int32)
    times = place // 128 * 256 + place % 128
    w0 = weights(block_starts, kept_freqs, times + side * 128)
    w1 = weights(block_starts, kept_freqs, times + (1 - side) * 128)
    first, w0, w1 = lax.optimization_barrier((first, w0, w1))
    first = exchange(first, PLANE)
    p0, p1 = partial(w0, x0, (low, LAST))
    s, g, part0 = middle(w1, passed, p0, own)
    s, g, part2 = whole(w0, w1, x0, first, g, s)
    s, t, part1 = rest(w1, last, p1, g, s, low, lax.axis_size(("y", "x")))
    t = exchange(t, ("y", "x")).sum(axis=0)
    t = to_all(t, ("zh", "zl", "c"))
    out = power(t, (part0, part1, part2), float(NB * total))
    shape = (1, NB, 2, NF, own)
    return s.reshape(shape), out.reshape(shape)


def solution(mesh):
    split = Mesh(mesh.devices.reshape(4, 2, 4, 2, mesh.shape["ga"]), ("y", "zh", "x", "c", "zl"))
    out = P("zl", None, None, None, TA)
    return jax.shard_map(
        shards, mesh=split, in_specs=(P(TA, "zl", None), P(), P()), out_specs=(out, out), check_vma=False
    )
```

profile of v0, /device:TPU:1, one launch (start us, length us, event | category | flops | bytes accessed | tf_op | source)
XLA Modules:
  0.0 173.6 jit_solution(1964513465980043059)
XLA Ops:
  0.6 2.7 %pack.4 = bf16[32,16,1408]{2,1,0:T(8,128)(2,1)} custom-call(bf16[16,131072]{1,0:T(8,128)(2,1)} %bitcast.10), custom_call_target="tpu_custom_call" | custom-call | tf_op jit(solution)/shard_map/pack/pallas_call | solution.py:74
  3.4 8.6 %all-to-all-start = ((bf16[32,16,1408]{2,1,0:T(8,128)(2,1)}), bf16[32,16,1408]{2,1,0:T(8,128)(2,1)S(1)}, u32[]{:S(2)}, u32[]{:S(2)}) async-start(bf16[32,16,1408]{2,1,0:T(8,128)(2,1)} %pack.4), calls=%async_computation | async-start | bytes 2883584 | tf_op jit(solution)/shard_map/all_to_all | solution.py:310
  12.0 3.2 %pack.5 = bf16[32,16,2048]{2,1,0:T(8,128)(2,1)} custom-call(bf16[16,131072]{1,0:T(8,128)(2,1)} %bitcast.11), custom_call_target="tpu_custom_call" | custom-call | tf_op jit(solution)/shard_map/pack/pallas_call | solution.py:74
  15.2 17.4 %all-to-all-done = bf16[32,16,1408]{2,1,0:T(8,128)(2,1)S(1)} async-done(((bf16[32,16,1408]{2,1,0:T(8,128)(2,1)}), bf16[32,16,1408]{2,1,0:T(8,128)(2,1)S(1)}, u32[]{:S(2)}, u32[]{:S(2)}) %all-to-all-start) | async-done | bytes 1441824 | tf_op jit(solution)/shard_map/all_to_all | solution.py:310
  32.5 5.5 %all-to-all-start.1 = ((bf16[32,16,2048]{2,1,0:T(8,128)(2,1)}), bf16[32,16,2048]{2,1,0:T(8,128)(2,1)S(1)}, u32[]{:S(2)}, u32[]{:S(2)}) async-start(bf16[32,16,2048]{2,1,0:T(8,128)(2,1)} %pack.5), calls=%async_computation.1 | async-start | bytes 4194304 | tf_op jit(solution)/shard_map/all_to_all | solution.py:310
  38.0 0.0 copy-start.9
  38.0 2.2 %pack.3 = bf16[32,16,640]{2,1,0:T(8,128)(2,1)} custom-call(bf16[16,131072]{1,0:T(8,128)(2,1)} %bitcast.12), custom_call_target="tpu_custom_call" | custom-call | tf_op jit(solution)/shard_map/pack/pallas_call | solution.py:74
  40.2 7.0 %collective-permute-start = (bf16[32,16,640]{2,1,0:T(8,128)(2,1)}, bf16[32,16,640]{2,1,0:T(8,128)(2,1)}, u32[]{:S(2)}, u32[]{:S(2)}) collective-permute-start(bf16[32,16,640]{2,1,0:T(8,128)(2,1)} %pack.3), channel_id=1, source_target_pairs={{0,32},{32,0},{1,33},{33,1},{2,34},{34,2},{3,35},{35,3},{4,36},{36... | collective-permute-start | bytes 1966088 | tf_op jit(solution)/shard_map/ppermute | solution.py:324
  47.3 0.2 fusion.15
  47.5 0.1 subtract_select_fusion
  47.5 1.0 slice.9
  48.6 0.0 collective-permute-start.2
  48.6 3.9 %multiply_convert_fusion.1 = (bf16[1,7,32,512]{3,2,1,0:T(8,128)(2,1)S(1)}, bf16[1,7,32,512]{3,2,1,0:T(8,128)(2,1)S(1)}, bf16[1,7,32,512]{3,2,1,0:T(8,128)(2,1)S(1)}, bf16[1,7,32,512]{3,2,1,0:T(8,128)(2,1)S(1)}) fusion(f32[7,512]{1,0:T(8,128)S(1)} %get-tuple-element.34, s32[7,512]{1,0:T(8,128)S(1)} %get-tuple-element.42, s32[32]{0:T(128)S(1)} %copy-done.10, ...), kind=kLoop, calls=%fused_computation.19 | loop fusion | flops 4587520 | bytes 1003648 | tf_op jit(solution)/shard_map/convert
  52.6 13.0 %collective-permute-done = bf16[32,16,640]{2,1,0:T(8,128)(2,1)} collective-permute-done((bf16[32,16,640]{2,1,0:T(8,128)(2,1)}, bf16[32,16,640]{2,1,0:T(8,128)(2,1)}, u32[]{:S(2)}, u32[]{:S(2)}) %collective-permute-start) | collective-permute-done | bytes 655392 | tf_op jit(solution)/shard_map/ppermute | solution.py:324
  65.6 1.1 all-to-all-done.1.x_ref.x0_ref
  66.7 7.7 %all-to-all-start.2 = ((bf16[32,16,640]{2,1,0:T(8,128)(2,1)}), bf16[32,16,640]{2,1,0:T(8,128)(2,1)}, u32[]{:S(2)}, u32[]{:S(2)}) async-start(bf16[32,16,640]{2,1,0:T(8,128)(2,1)} %collective-permute-done), calls=%async_computation.2 | async-start | bytes 1310720 | tf_op jit(solution)/shard_map/all_to_all | solution.py:310
  74.4 1.9 %slice.8 = bf16[32,16,512]{2,1,0:T(8,128)(2,1)} slice(bf16[32,16,1408]{2,1,0:T(8,128)(2,1)} %copy-done.8), slice={[0:32], [0:16], [896:1408]} | slice | bytes 1048576 | tf_op jit(solution)/shard_map/slice | solution.py:328
  76.3 5.8 %collective-permute-start.1 = (bf16[32,16,512]{2,1,0:T(8,128)(2,1)}, bf16[32,16,512]{2,1,0:T(8,128)(2,1)S(1)}, u32[]{:S(2)}, u32[]{:S(2)}) collective-permute-start(bf16[32,16,512]{2,1,0:T(8,128)(2,1)} %slice.8), channel_id=1, source_target_pairs={{0,32},{32,0},{1,33},{33,1},{2,34},{34,2},{3,35},{35,3},{4,36},{36... | collective-permute-start | bytes 1572872 | tf_op jit(solution)/shard_map/ppermute | solution.py:328
  82.1 0.9 partial.1
  83.0 0.9 copy-done
  83.9 8.8 %collective-permute-done.2.x_ref = bf16[32,16,896]{2,1,0:T(8,128)(2,1)} collective-permute-done((bf16[32,16,896]{2,1,0:T(8,128)(2,1)}, bf16[32,16,896]{2,1,0:T(8,128)(2,1)}, u32[]{:S(2)}, u32[]{:S(2)}) %collective-permute-start.2) | collective-permute-done | bytes 917536 | tf_op jit(solution)/shard_map/ppermute | solution.py:327
  92.6 2.8 %middle.1 = (bf16[448,2048]{1,0:T(8,128)(2,1)}, f32[448,224]{1,0:T(8,128)S(1)}, bf16[448,896]{1,0:T(8,128)(2,1)S(1)}) custom-call(bf16[448,512]{1,0:T(8,128)(2,1)S(1)} %bitcast.5, bf16[32,16,896]{2,1,0:T(8,128)(2,1)} %collective-permute-done.2.x_ref, f32[448,896]{1,0:T(8,128)S(1)} %get-tuple-element.20.p_ref), custom_call_target="tpu_custom_call" | custom-call | flops 411041792 | bytes 4194304 | tf_op jit(solution)/shard_map/middle/pallas_call | solution.py:181
  95.5 0.9 copy-done.2
  96.4 0.8 copy-done.6
  97.2 1.0 copy-done.7
  98.2 3.1 %whole.1 = (bf16[448,2048]{1,0:T(8,128)(2,1)}, f32[448,224]{1,0:T(8,128)S(1)}, bf16[448,640]{1,0:T(8,128)(2,1)S(1)}) custom-call(bf16[448,512]{1,0:T(8,128)(2,1)S(1)} %bitcast.9, bf16[448,512]{1,0:T(8,128)(2,1)S(1)} %bitcast.6, bf16[32,16,2048]{2,1,0:T(8,128)(2,1)S(1)} %all-to-all-done.1.x_ref.x0_ref, ...), custom_call_target="tpu_custom_call", output_to_operand_aliasing={{0}: (5, {})} | custom-call | flops 587202560 | bytes 4194304 | tf_op jit(solution)/shard_map/whole/pallas_call | solution.py:118
  101.3 0.8 copy-done.4
  102.2 7.1 %collective-permute-done.1.x_ref = bf16[32,16,512]{2,1,0:T(8,128)(2,1)S(1)} collective-permute-done((bf16[32,16,512]{2,1,0:T(8,128)(2,1)}, bf16[32,16,512]{2,1,0:T(8,128)(2,1)S(1)}, u32[]{:S(2)}, u32[]{:S(2)}) %collective-permute-start.1) | collective-permute-done | bytes 524320 | tf_op jit(solution)/shard_map/ppermute | solution.py:328
  109.3 1.4 rest.1
  110.7 13.4 %all_to_all.25 = f32[16,8,256]{2,1,0:T(8,128)S(1)} all-to-all(f32[16,8,256]{2,1,0:T(8,128)S(1)} %get-tuple-element.26), channel_id=1, replica_groups=mesh['y'=4,'zh'=2,'x'=4,'c'=2,'zl'=4] {'y','x'}, dimensions={0} | all-to-all | bytes 262144 | tf_op jit(solution)/shard_map/all_to_all | solution.py:310
  124.1 46.6 %all_to_all.26.t_ref = f32[16,8,256]{2,1,0:T(8,128)S(1)} all-to-all(f32[16,8,256]{2,1,0:T(8,128)S(1)} %broadcast_in_dim.11), channel_id=1, replica_groups=mesh['y'=4,'zh'=2,'x'=4,'c'=2,'zl'=4] {'zh','zl','c'}, dimensions={0} | all-to-all | bytes 262144 | tf_op jit(solution)/shard_map/all_to_all | solution.py:306
  170.7 2.9 %power.1 = f32[448,2048]{1,0:T(8,128)} custom-call(f32[16,8,256]{2,1,0:T(8,128)S(1)} %all_to_all.26.t_ref, bf16[448,896]{1,0:T(8,128)(2,1)S(1)} %copy-done.3, bf16[448,512]{1,0:T(8,128)(2,1)S(1)} %get-tuple-element.28.refs_1_, bf16[448,640]{1,0:T(8,128)(2,1)S(1)} %copy-done.5), custom_call_target="tpu_custom_call" | custom-call | tf_op jit(solution)/shard_map/power/pallas_call | solution.py:289
  (22 shorter events, 0.2 us)
Async XLA Ops:
  3.4 29.2 %all-to-all-start = ((bf16[32,16,1408]{2,1,0:T(8,128)(2,1)}), bf16[32,16,1408]{2,1,0:T(8,128)(2,1)S(1)}, u32[]{:S(2)}, u32[]{:S(2)}) async-start(bf16[32,16,1408]{2,1,0:T(8,128)(2,1)} %pack.4), calls=%async_computation | async-start | bytes 2883584 | tf_op jit(solution)/shard_map/all_to_all | solution.py:310
  32.5 15.0 %copy-start.8 = (bf16[32,16,1408]{2,1,0:T(8,128)(2,1)}, bf16[32,16,1408]{2,1,0:T(8,128)(2,1)S(1)}, u32[]{:S(2)}) copy-start(bf16[32,16,1408]{2,1,0:T(8,128)(2,1)S(1)} %all-to-all-done) | copy-start | bytes 4325380
  32.5 34.2 %all-to-all-start.1 = ((bf16[32,16,2048]{2,1,0:T(8,128)(2,1)}), bf16[32,16,2048]{2,1,0:T(8,128)(2,1)S(1)}, u32[]{:S(2)}, u32[]{:S(2)}) async-start(bf16[32,16,2048]{2,1,0:T(8,128)(2,1)} %pack.5), calls=%async_computation.1 | async-start | bytes 4194304 | tf_op jit(solution)/shard_map/all_to_all | solution.py:310
  38.0 9.2 %copy-start.9 = (s32[7]{0:T(128)S(1)}, s32[7]{0:T(128)}, u32[]{:S(2)}) copy-start(s32[7]{0:T(128)} %param.4) | copy-start | bytes 88
  40.2 8.4 %copy-start.10 = (s32[32]{0:T(128)S(1)}, s32[32]{0:T(128)}, u32[]{:S(2)}) copy-start(s32[32]{0:T(128)} %param.5) | copy-start | bytes 388
  40.2 25.4 %collective-permute-start = (bf16[32,16,640]{2,1,0:T(8,128)(2,1)}, bf16[32,16,640]{2,1,0:T(8,128)(2,1)}, u32[]{:S(2)}, u32[]{:S(2)}) collective-permute-start(bf16[32,16,640]{2,1,0:T(8,128)(2,1)} %pack.3), channel_id=1, source_target_pairs={{0,32},{32,0},{1,33},{33,1},{2,34},{34,2},{3,35},{35,3},{4,36},{36... | collective-permute-start | bytes 1966088 | tf_op jit(solution)/shard_map/ppermute | solution.py:324
  48.6 44.1 %collective-permute-start.2 = (bf16[32,16,896]{2,1,0:T(8,128)(2,1)}, bf16[32,16,896]{2,1,0:T(8,128)(2,1)}, u32[]{:S(2)}, u32[]{:S(2)}) collective-permute-start(bf16[32,16,896]{2,1,0:T(8,128)(2,1)} %slice.9), channel_id=1, source_target_pairs={{0,32},{32,0},{1,33},{33,1},{2,34},{34,2},{3,35},{35,3},{4,36},{36... | collective-permute-start | bytes 2752520 | tf_op jit(solution)/shard_map/ppermute | solution.py:327
  66.7 30.4 %all-to-all-start.2 = ((bf16[32,16,640]{2,1,0:T(8,128)(2,1)}), bf16[32,16,640]{2,1,0:T(8,128)(2,1)}, u32[]{:S(2)}, u32[]{:S(2)}) async-start(bf16[32,16,640]{2,1,0:T(8,128)(2,1)} %collective-permute-done), calls=%async_computation.2 | async-start | bytes 1310720 | tf_op jit(solution)/shard_map/all_to_all | solution.py:310
  76.3 33.0 %collective-permute-start.1 = (bf16[32,16,512]{2,1,0:T(8,128)(2,1)}, bf16[32,16,512]{2,1,0:T(8,128)(2,1)S(1)}, u32[]{:S(2)}, u32[]{:S(2)}) collective-permute-start(bf16[32,16,512]{2,1,0:T(8,128)(2,1)} %slice.8), channel_id=1, source_target_pairs={{0,32},{32,0},{1,33},{33,1},{2,34},{34,2},{3,35},{35,3},{4,36},{36... | collective-permute-start | bytes 1572872 | tf_op jit(solution)/shard_map/ppermute | solution.py:328
  83.0 0.9 copy-start
  95.5 0.9 copy-start.2
  96.4 0.8 copy-start.6
  97.2 1.0 copy-start.7
  98.2 11.1 %copy-start.1 = (f32[448,512]{1,0:T(8,128)S(1)}, f32[448,512]{1,0:T(8,128)}, u32[]{:S(2)}) copy-start(f32[448,512]{1,0:T(8,128)} %copy-done) | copy-start | bytes 2752516
  101.3 0.9 copy-start.4
  109.3 61.4 %copy-start.3 = (bf16[448,896]{1,0:T(8,128)(2,1)S(1)}, bf16[448,896]{1,0:T(8,128)(2,1)}, u32[]{:S(2)}) copy-start(bf16[448,896]{1,0:T(8,128)(2,1)} %copy-done.2) | copy-start | bytes 2408452
  109.3 61.4 %copy-start.5 = (bf16[448,640]{1,0:T(8,128)(2,1)S(1)}, bf16[448,640]{1,0:T(8,128)(2,1)}, u32[]{:S(2)}) copy-start(bf16[448,640]{1,0:T(8,128)(2,1)} %copy-done.4) | copy-start | bytes 1720324
where the time goes:
time: 174 us
  blocking collectives  60 us (34%)
  waiting for transfers between devices  47.3 us (27%)
  starting transfers between devices  34.6 us (20%)
  Pallas kernels  19.2 us (11%)
  local copies, waits for them, and re-layouts  7.38 us (4%)
  other arithmetic  4.33 us (2%)
    all_to_all x1, blocking collectives, to_all(): return lax.all_to_all(copies, axes, 0, 0, tiled=True)  46.6 us
    all_to_all x3, starting transfers between devices, exchange(): return lax.all_to_all(x, axes, 0, 0, tiled=True)  21.8 us
    all_to_all x3, waiting for transfers between devices, exchange(): return lax.all_to_all(x, axes, 0, 0, tiled=True)  18.5 us
    all_to_all x1, blocking collectives, exchange(): return lax.all_to_all(x, axes, 0, 0, tiled=True)  13.4 us
    ppermute x1, waiting for transfers between devices, shards(): first = lax.ppermute(first, 'zh', swap)  13 us
    ppermute x1, waiting for transfers between devices, shards(): passed = lax.ppermute(pass_on[:, :, :low], 'zh', swap)  8.75 us
    pallas_call x3, Pallas kernels, pack(): pl.pallas_call(functools.partial(pack_kernel, own, [job[:2] for job in jo...  8.1 us
    ppermute x1, waiting for transfers between devices, shards(): last = lax.ppermute(pass_on[:, :, low:], 'zh', swap)  7.12 us
  transfers between devices with their start and end apart: 6, of which 5 were waited for; matrix products, arithmetic and copies ran while one was open for 4% of the time, Pallas kernels for 7%

commit v1 on v0

--- a/solution.py
+++ b/solution.py
@@ -18,7 +18,7 @@
 PAIRS = NB // 2
 TA = ("y", "zh", "x", "c")
 PLANE = ("y", "x", "c")
-FIRST = 640
+FIRST = 768
 LAST = 512
 F32 = jnp.float32
 BF16 = jnp.bfloat16
@@ -98,7 +98,7 @@
     return ref[...].reshape(-1, ref.shape[2])
 
 
-def whole_kernel(w0_ref, w1_ref, x0_ref, x1_ref, g_ref, _, s_ref, out_ref, part_ref, sem):
+def whole_kernel(w0_ref, w1_ref, x0_ref, x1_ref, _, s_ref, out_ref, part_ref, sem):
     count = x1_ref.shape[2]
     low = x0_ref.shape[2] - count
     near = x0_ref[:, :, low:].reshape(-1, count)
@@ -106,11 +106,11 @@
     emit(parts, part_ref)
     save = pltpu.make_async_copy(part_ref, s_ref.at[:, pl.ds(low, count)], sem)
     save.start()
-    out_ref[...] = g_ref[...] + gram_of(parts)
+    out_ref[...] = gram_of(parts)
     save.wait()
 
 
-def whole(w0, w1, x0, x1, g, s):
+def whole(w0, w1, x0, x1, s):
     times = w0.shape[1]
     count = x1.shape[2]
     here = pl.BlockSpec(memory_space=pltpu.VMEM)
@@ -122,14 +122,14 @@
             jax.ShapeDtypeStruct((ROWS, HALF), F32),
             jax.ShapeDtypeStruct((ROWS, count), BF16),
         ),
-        in_specs=[here] * 5 + [there],
+        in_specs=[here] * 4 + [there],
         out_specs=(there, here, here),
         scratch_shapes=[pltpu.SemaphoreType.DMA],
-        input_output_aliases={5: 0},
+        input_output_aliases={4: 0},
         compiler_params=pltpu.CompilerParams(vmem_limit_bytes=16 * 2**20),
         cost_estimate=pl.CostEstimate(flops=4 * ROWS * times * count, bytes_accessed=2**22, transcendentals=0),
         name="whole",
-    )(w0, w1, x0, x1, g, s)
+    )(w0, w1, x0, x1, s)
 
 
 def partial_kernel(w_ref, x_ref, *p_refs):
@@ -194,13 +194,13 @@
     )(w, x, p)
 
 
-def rest_kernel(low, w_ref, x_ref, p_ref, g_ref, _, s_ref, t_ref, part_ref, row_ref, sem):
+def rest_kernel(low, w_ref, x_ref, p_ref, g0_ref, g1_ref, _, s_ref, t_ref, part_ref, row_ref, sem):
     width = x_ref.shape[2]
     parts = (p_ref[...] + dot(w_ref[...], rows_of(x_ref))).astype(BF16)
     emit(parts, part_ref)
     save = pltpu.make_async_copy(part_ref, s_ref.at[:, pl.ds(low, width)], sem)
     save.start()
-    kept = jnp.where(same_freq(ROWS), g_ref[...] + gram_of(parts), 0.0)
+    kept = jnp.where(same_freq(ROWS), g0_ref[...] + g1_ref[...] + gram_of(parts), 0.0)
     tables = kept.reshape(2 * NB, NF, HALF).sum(axis=1)
     block = lax.broadcasted_iota(jnp.int32, (NB, HALF), 0)
     row_ref[...] = jnp.zeros_like(row_ref)
@@ -218,7 +218,7 @@
     save.wait()
 
 
-def rest(w, x, p, g, s, low, copies):
+def rest(w, x, p, g0, g1, s, low, copies):
     times = w.shape[1]
     width = x.shape[2]
     here = pl.BlockSpec(memory_space=pltpu.VMEM)
@@ -230,14 +230,14 @@
             jax.ShapeDtypeStruct((copies, 8, 256), F32),
             jax.ShapeDtypeStruct((ROWS, width), BF16),
         ),
-        in_specs=[here, here, here, here, there],
+        in_specs=[here] * 5 + [there],
         out_specs=(there, here, here),
         scratch_shapes=[pltpu.VMEM((16, 256), F32), pltpu.SemaphoreType.DMA],
-        input_output_aliases={4: 0},
+        input_output_aliases={5: 0},
         compiler_params=pltpu.CompilerParams(vmem_limit_bytes=16 * 2**20),
         cost_estimate=pl.CostEstimate(flops=2 * ROWS * times * width, bytes_accessed=2**22, transcendentals=0),
         name="rest",
-    )(w, x, p, g, s)
+    )(w, x, p, g0, g1, s)
 
 
 def spread_to(part):
@@ -336,9 +336,9 @@
     first, w0, w1 = lax.optimization_barrier((first, w0, w1))
     first = exchange(first, PLANE)
     p0, p1 = partial(w0, x0, (low, LAST))
-    s, g, part0 = middle(w1, passed, p0, own)
-    s, g, part2 = whole(w0, w1, x0, first, g, s)
-    s, t, part1 = rest(w1, last, p1, g, s, low, lax.axis_size(("y", "x")))
+    s, g0, part0 = middle(w1, passed, p0, own)
+    s, g1, part2 = whole(w0, w1, x0, first, s)
+    s, t, part1 = rest(w1, last, p1, g0, g1, s, low, lax.axis_size(("y", "x")))
     t = exchange(t, ("y", "x")).sum(axis=0)
     t = to_all(t, ("zh", "zl", "c"))
     out = power(t, (part0, part1, part2), float(NB * total))

time: 174 us -> 174 us (level)
  waiting for transfers between devices: 47.3 us -> 43.9 us
  starting transfers between devices: 34.6 us -> 36.7 us
    ppermute x1, waiting for transfers between devices: 8.75 us -> 4.72 us  [shards(): passed = lax.ppermute(pass_on[:, :, :low], 'zh', swap)]
    all_to_all x3, waiting for transfers between devices: 18.5 us -> 16.1 us  [exchange(): return lax.all_to_all(x, axes, 0, 0, tiled=True)]
    all_to_all x3, starting transfers between devices: 21.8 us -> 23.8 us  [exchange(): return lax.all_to_all(x, axes, 0, 0, tiled=True)]
    ppermute x1, waiting for transfers between devices: 13 us -> 14.8 us  [shards(): first = lax.ppermute(first, 'zh', swap)]
  transfers between devices with their start and end apart: 6 -> 6, of which waited for: 5 -> 4; matrix products, arithmetic and copies ran while one was open for 4% -> 5% of each run, Pallas kernels for 7% -> 7%
where the time goes in v1:
time: 174 us; the launch traced here: 173 us
  blocking collectives  60 us (34%)
  waiting for transfers between devices  43.9 us (25%)
  starting transfers between devices  36.7 us (21%)
  Pallas kernels  19 us (11%)
  local copies, waits for them, and re-layouts  8.42 us (5%)
  other arithmetic  4.34 us (2%)
    all_to_all x1, blocking collectives, to_all(): return lax.all_to_all(copies, axes, 0, 0, tiled=True)  46.6 us
    all_to_all x3, starting transfers between devices, exchange(): return lax.all_to_all(x, axes, 0, 0, tiled=True)  23.8 us
    all_to_all x3, waiting for transfers between devices, exchange(): return lax.all_to_all(x, axes, 0, 0, tiled=True)  16.1 us
    ppermute x1, waiting for transfers between devices, shards(): first = lax.ppermute(first, 'zh', swap)  14.8 us
    all_to_all x1, blocking collectives, exchange(): return lax.all_to_all(x, axes, 0, 0, tiled=True)  13.4 us
    ppermute x1, waiting for transfers between devices, shards(): last = lax.ppermute(pass_on[:, :, low:], 'zh', swap)  8.27 us
    pallas_call x3, Pallas kernels, pack(): pl.pallas_call(functools.partial(pack_kernel, own, [job[:2] for job in jo...  8.15 us
    ppermute x1, starting transfers between devices, shards(): first = lax.ppermute(first, 'zh', swap)  7 us
  transfers between devices with their start and end apart: 6, of which 4 were waited for; matrix products, arithmetic and copies ran while one was open for 5% of the time, Pallas kernels for 7%

profile of v1, /device:TPU:1, one launch (start us, length us, event | category | flops | bytes accessed | tf_op | source)
XLA Modules:
  0.0 173.0 jit_solution(16910847514205718695)
XLA Ops:
  0.6 2.6 %pack.4 = bf16[32,16,1280]{2,1,0:T(8,128)(2,1)} custom-call(bf16[16,131072]{1,0:T(8,128)(2,1)} %bitcast.10), custom_call_target="tpu_custom_call" | custom-call | tf_op jit(solution)/shard_map/pack/pallas_call | solution.py:74
  3.3 8.6 %all-to-all-start = ((bf16[32,16,1280]{2,1,0:T(8,128)(2,1)}), bf16[32,16,1280]{2,1,0:T(8,128)(2,1)S(1)}, u32[]{:S(2)}, u32[]{:S(2)}) async-start(bf16[32,16,1280]{2,1,0:T(8,128)(2,1)} %pack.4), calls=%async_computation | async-start | bytes 2621440 | tf_op jit(solution)/shard_map/all_to_all | solution.py:310
  11.9 3.2 %pack.5 = bf16[32,16,2048]{2,1,0:T(8,128)(2,1)} custom-call(bf16[16,131072]{1,0:T(8,128)(2,1)} %bitcast.11), custom_call_target="tpu_custom_call" | custom-call | tf_op jit(solution)/shard_map/pack/pallas_call | solution.py:74
  15.1 16.1 %all-to-all-done = bf16[32,16,1280]{2,1,0:T(8,128)(2,1)S(1)} async-done(((bf16[32,16,1280]{2,1,0:T(8,128)(2,1)}), bf16[32,16,1280]{2,1,0:T(8,128)(2,1)S(1)}, u32[]{:S(2)}, u32[]{:S(2)}) %all-to-all-start) | async-done | bytes 1310752 | tf_op jit(solution)/shard_map/all_to_all | solution.py:310
  31.1 1.1 copy-done.8
  32.2 5.2 %all-to-all-start.1 = ((bf16[32,16,2048]{2,1,0:T(8,128)(2,1)}), bf16[32,16,2048]{2,1,0:T(8,128)(2,1)S(1)}, u32[]{:S(2)}, u32[]{:S(2)}) async-start(bf16[32,16,2048]{2,1,0:T(8,128)(2,1)} %pack.5), calls=%async_computation.1 | async-start | bytes 4194304 | tf_op jit(solution)/shard_map/all_to_all | solution.py:310
  37.4 0.0 copy-start.9
  37.4 0.0 copy-start.10
  37.4 2.3 %pack.3 = bf16[32,16,768]{2,1,0:T(8,128)(2,1)} custom-call(bf16[16,131072]{1,0:T(8,128)(2,1)} %bitcast.12), custom_call_target="tpu_custom_call" | custom-call | tf_op jit(solution)/shard_map/pack/pallas_call | solution.py:74
  39.7 7.0 %collective-permute-start = (bf16[32,16,768]{2,1,0:T(8,128)(2,1)}, bf16[32,16,768]{2,1,0:T(8,128)(2,1)}, u32[]{:S(2)}, u32[]{:S(2)}) collective-permute-start(bf16[32,16,768]{2,1,0:T(8,128)(2,1)} %pack.3), channel_id=1, source_target_pairs={{0,32},{32,0},{1,33},{33,1},{2,34},{34,2},{3,35},{35,3},{4,36},{36... | collective-permute-start | bytes 2359304 | tf_op jit(solution)/shard_map/ppermute | solution.py:324
  46.7 0.1 subtract_select_fusion
  46.8 0.2 fusion.15
  47.0 4.0 %multiply_convert_fusion.1 = (bf16[1,7,32,512]{3,2,1,0:T(8,128)(2,1)S(1)}, bf16[1,7,32,512]{3,2,1,0:T(8,128)(2,1)S(1)}, bf16[1,7,32,512]{3,2,1,0:T(8,128)(2,1)S(1)}, bf16[1,7,32,512]{3,2,1,0:T(8,128)(2,1)S(1)}) fusion(f32[7,512]{1,0:T(8,128)S(1)} %get-tuple-element.34, s32[7,512]{1,0:T(8,128)S(1)} %get-tuple-element.42, s32[32]{0:T(128)S(1)} %copy-done.10, ...), kind=kLoop, calls=%fused_computation.19 | loop fusion | flops 4587520 | bytes 1003648 | tf_op jit(solution)/shard_map/convert
  51.0 2.1 %slice.9 = bf16[32,16,768]{2,1,0:T(8,128)(2,1)} slice(bf16[32,16,1280]{2,1,0:T(8,128)(2,1)} %copy-done.8), slice={[0:32], [0:16], [0:768]} | slice | bytes 1572864 | tf_op jit(solution)/shard_map/slice | solution.py:327
  53.1 0.0 collective-permute-start.2
  53.2 14.8 %collective-permute-done = bf16[32,16,768]{2,1,0:T(8,128)(2,1)} collective-permute-done((bf16[32,16,768]{2,1,0:T(8,128)(2,1)}, bf16[32,16,768]{2,1,0:T(8,128)(2,1)}, u32[]{:S(2)}, u32[]{:S(2)}) %collective-permute-start) | collective-permute-done | bytes 786464 | tf_op jit(solution)/shard_map/ppermute | solution.py:324
  68.0 10.1 %all-to-all-start.2 = ((bf16[32,16,768]{2,1,0:T(8,128)(2,1)}), bf16[32,16,768]{2,1,0:T(8,128)(2,1)}, u32[]{:S(2)}, u32[]{:S(2)}) async-start(bf16[32,16,768]{2,1,0:T(8,128)(2,1)} %collective-permute-done), calls=%async_computation.2 | async-start | bytes 1572864 | tf_op jit(solution)/shard_map/all_to_all | solution.py:310
  78.0 1.9 %slice.8 = bf16[32,16,512]{2,1,0:T(8,128)(2,1)} slice(bf16[32,16,1280]{2,1,0:T(8,128)(2,1)} %copy-done.8), slice={[0:32], [0:16], [768:1280]} | slice | bytes 1048576 | tf_op jit(solution)/shard_map/slice | solution.py:328
  79.9 5.8 %collective-permute-start.1 = (bf16[32,16,512]{2,1,0:T(8,128)(2,1)}, bf16[32,16,512]{2,1,0:T(8,128)(2,1)S(1)}, u32[]{:S(2)}, u32[]{:S(2)}) collective-permute-start(bf16[32,16,512]{2,1,0:T(8,128)(2,1)} %slice.8), channel_id=1, source_target_pairs={{0,32},{32,0},{1,33},{33,1},{2,34},{34,2},{3,35},{35,3},{4,36},{36... | collective-permute-start | bytes 1572872 | tf_op jit(solution)/shard_map/ppermute | solution.py:328
  85.7 0.8 partial.1
  86.5 0.9 copy-done
  87.4 4.7 %collective-permute-done.2.x_ref = bf16[32,16,768]{2,1,0:T(8,128)(2,1)} collective-permute-done((bf16[32,16,768]{2,1,0:T(8,128)(2,1)}, bf16[32,16,768]{2,1,0:T(8,128)(2,1)}, u32[]{:S(2)}, u32[]{:S(2)}) %collective-permute-start.2) | collective-permute-done | bytes 786464 | tf_op jit(solution)/shard_map/ppermute | solution.py:327
  92.1 2.6 %middle.1 = (bf16[448,2048]{1,0:T(8,128)(2,1)}, f32[448,224]{1,0:T(8,128)S(1)}, bf16[448,768]{1,0:T(8,128)(2,1)S(1)}) custom-call(bf16[448,512]{1,0:T(8,128)(2,1)S(1)} %bitcast.5, bf16[32,16,768]{2,1,0:T(8,128)(2,1)} %collective-permute-done.2.x_ref, f32[448,768]{1,0:T(8,128)S(1)} %get-tuple-element.19.p_ref), custom_call_target="tpu_custom_call" | custom-call | flops 352321536 | bytes 4194304 | tf_op jit(solution)/shard_map/middle/pallas_call | solution.py:181
  94.8 0.8 copy-done.2
  95.6 0.8 copy-done.6
  96.4 3.2 %whole.1 = (bf16[448,2048]{1,0:T(8,128)(2,1)}, f32[448,224]{1,0:T(8,128)S(1)}, bf16[448,768]{1,0:T(8,128)(2,1)S(1)}) custom-call(bf16[448,512]{1,0:T(8,128)(2,1)S(1)} %bitcast.9, bf16[448,512]{1,0:T(8,128)(2,1)S(1)} %bitcast.6, bf16[32,16,2048]{2,1,0:T(8,128)(2,1)S(1)} %all-to-all-done.1.x_ref.x0_ref, ...), custom_call_target="tpu_custom_call", output_to_operand_aliasing={{0}: (4, {})} | custom-call | flops 704643072 | bytes 4194304 | tf_op jit(solution)/shard_map/whole/pallas_call | solution.py:118
  99.6 0.8 copy-done.4
  100.5 8.3 %collective-permute-done.1.x_ref = bf16[32,16,512]{2,1,0:T(8,128)(2,1)S(1)} collective-permute-done((bf16[32,16,512]{2,1,0:T(8,128)(2,1)}, bf16[32,16,512]{2,1,0:T(8,128)(2,1)S(1)}, u32[]{:S(2)}, u32[]{:S(2)}) %collective-permute-start.1) | collective-permute-done | bytes 524320 | tf_op jit(solution)/shard_map/ppermute | solution.py:328
  108.8 1.4 rest.1
  110.2 13.4 %all_to_all.25 = f32[16,8,256]{2,1,0:T(8,128)S(1)} all-to-all(f32[16,8,256]{2,1,0:T(8,128)S(1)} %get-tuple-element.26), channel_id=1, replica_groups=mesh['y'=4,'zh'=2,'x'=4,'c'=2,'zl'=4] {'y','x'}, dimensions={0} | all-to-all | bytes 262144 | tf_op jit(solution)/shard_map/all_to_all | solution.py:310
  123.6 46.6 %all_to_all.26.t_ref = f32[16,8,256]{2,1,0:T(8,128)S(1)} all-to-all(f32[16,8,256]{2,1,0:T(8,128)S(1)} %broadcast_in_dim.11), channel_id=1, replica_groups=mesh['y'=4,'zh'=2,'x'=4,'c'=2,'zl'=4] {'zh','zl','c'}, dimensions={0} | all-to-all | bytes 262144 | tf_op jit(solution)/shard_map/all_to_all | solution.py:306
  170.2 2.8 %power.1 = f32[448,2048]{1,0:T(8,128)} custom-call(f32[16,8,256]{2,1,0:T(8,128)S(1)} %all_to_all.26.t_ref, bf16[448,768]{1,0:T(8,128)(2,1)S(1)} %copy-done.3, bf16[448,512]{1,0:T(8,128)(2,1)S(1)} %get-tuple-element.28.refs_1_, bf16[448,768]{1,0:T(8,128)(2,1)S(1)} %copy-done.5), custom_call_target="tpu_custom_call" | custom-call | tf_op jit(solution)/shard_map/power/pallas_call | solution.py:289
  (22 shorter events, 0.2 us)
Async XLA Ops:
  3.3 27.9 %all-to-all-start = ((bf16[32,16,1280]{2,1,0:T(8,128)(2,1)}), bf16[32,16,1280]{2,1,0:T(8,128)(2,1)S(1)}, u32[]{:S(2)}, u32[]{:S(2)}) async-start(bf16[32,16,1280]{2,1,0:T(8,128)(2,1)} %pack.4), calls=%async_computation | async-start | bytes 2621440 | tf_op jit(solution)/shard_map/all_to_all | solution.py:310
  31.1 1.1 copy-start.8
  32.2 35.8 %all-to-all-start.1 = ((bf16[32,16,2048]{2,1,0:T(8,128)(2,1)}), bf16[32,16,2048]{2,1,0:T(8,128)(2,1)S(1)}, u32[]{:S(2)}, u32[]{:S(2)}) async-start(bf16[32,16,2048]{2,1,0:T(8,128)(2,1)} %pack.5), calls=%async_computation.1 | async-start | bytes 4194304 | tf_op jit(solution)/shard_map/all_to_all | solution.py:310
  37.4 9.4 %copy-start.9 = (s32[7]{0:T(128)S(1)}, s32[7]{0:T(128)}, u32[]{:S(2)}) copy-start(s32[7]{0:T(128)} %param.4) | copy-start | bytes 88
  37.4 9.6 %copy-start.10 = (s32[32]{0:T(128)S(1)}, s32[32]{0:T(128)}, u32[]{:S(2)}) copy-start(s32[32]{0:T(128)} %param.5) | copy-start | bytes 388
  39.7 28.2 %collective-permute-start = (bf16[32,16,768]{2,1,0:T(8,128)(2,1)}, bf16[32,16,768]{2,1,0:T(8,128)(2,1)}, u32[]{:S(2)}, u32[]{:S(2)}) collective-permute-start(bf16[32,16,768]{2,1,0:T(8,128)(2,1)} %pack.3), channel_id=1, source_target_pairs={{0,32},{32,0},{1,33},{33,1},{2,34},{34,2},{3,35},{35,3},{4,36},{36... | collective-permute-start | bytes 2359304 | tf_op jit(solution)/shard_map/ppermute | solution.py:324
  53.1 39.0 %collective-permute-start.2 = (bf16[32,16,768]{2,1,0:T(8,128)(2,1)}, bf16[32,16,768]{2,1,0:T(8,128)(2,1)}, u32[]{:S(2)}, u32[]{:S(2)}) collective-permute-start(bf16[32,16,768]{2,1,0:T(8,128)(2,1)} %slice.9), channel_id=1, source_target_pairs={{0,32},{32,0},{1,33},{33,1},{2,34},{34,2},{3,35},{35,3},{4,36},{36... | collective-permute-start | bytes 2359304 | tf_op jit(solution)/shard_map/ppermute | solution.py:327
  68.0 28.4 %all-to-all-start.2 = ((bf16[32,16,768]{2,1,0:T(8,128)(2,1)}), bf16[32,16,768]{2,1,0:T(8,128)(2,1)}, u32[]{:S(2)}, u32[]{:S(2)}) async-start(bf16[32,16,768]{2,1,0:T(8,128)(2,1)} %collective-permute-done), calls=%async_computation.2 | async-start | bytes 1572864 | tf_op jit(solution)/shard_map/all_to_all | solution.py:310
  79.9 28.9 %collective-permute-start.1 = (bf16[32,16,512]{2,1,0:T(8,128)(2,1)}, bf16[32,16,512]{2,1,0:T(8,128)(2,1)S(1)}, u32[]{:S(2)}, u32[]{:S(2)}) collective-permute-start(bf16[32,16,512]{2,1,0:T(8,128)(2,1)} %slice.8), channel_id=1, source_target_pairs={{0,32},{32,0},{1,33},{33,1},{2,34},{34,2},{3,35},{35,3},{4,36},{36... | collective-permute-start | bytes 1572872 | tf_op jit(solution)/shard_map/ppermute | solution.py:328
  86.5 0.9 copy-start
  94.8 0.8 copy-start.2
  95.6 0.8 copy-start.6
  96.4 12.4 %copy-start.1 = (f32[448,512]{1,0:T(8,128)S(1)}, f32[448,512]{1,0:T(8,128)}, u32[]{:S(2)}) copy-start(f32[448,512]{1,0:T(8,128)} %copy-done) | copy-start | bytes 2752516
  96.4 12.4 %copy-start.7 = (f32[448,224]{1,0:T(8,128)S(1)}, f32[448,224]{1,0:T(8,128)}, u32[]{:S(2)}) copy-start(f32[448,224]{1,0:T(8,128)} %copy-done.6) | copy-start | bytes 1204228
  99.6 0.9 copy-start.4
  108.8 61.4 %copy-start.3 = (bf16[448,768]{1,0:T(8,128)(2,1)S(1)}, bf16[448,768]{1,0:T(8,128)(2,1)}, u32[]{:S(2)}) copy-start(bf16[448,768]{1,0:T(8,128)(2,1)} %copy-done.2) | copy-start | bytes 2064388
  108.8 61.4 %copy-start.5 = (bf16[448,768]{1,0:T(8,128)(2,1)S(1)}, bf16[448,768]{1,0:T(8,128)(2,1)}, u32[]{:S(2)}) copy-start(bf16[448,768]{1,0:T(8,128)(2,1)} %copy-done.4) | copy-start | bytes 2064388

commit v2 on v1

--- a/solution.py
+++ b/solution.py
@@ -52,31 +52,38 @@
     return row % NF == col % NF
 
 
-def pack_kernel(own, jobs, x_ref, *refs):
-    outs, sems = refs[:-1], refs[-1]
-    me = lax.axis_index("zh")
-    copies = []
-    for out, (shift, low) in zip(outs, jobs):
-        side = (me + shift) % 2
-        for d in range(out.shape[0]):
-            start = ((d // 8) * 16 + d % 8) * own + low + side * (8 * own)
-            cols = pl.ds(pl.multiple_of(start, 128), out.shape[2])
-            copies.append(pltpu.make_async_copy(x_ref.at[:, cols], out.at[d], sems.at[len(copies)]))
-    for copy in copies:
-        copy.start()
-    for copy in copies:
-        copy.wait()
-
-
-def pack(x, own, jobs):
+def pack_kernel(own, shift, low, x_ref, out_ref, buffer, in_sem, out_sem):
+    side = (lax.axis_index("zh") + shift) % 2
+    loads = []
+    for d in range(buffer.shape[0]):
+        start = ((d // 8) * 16 + d % 8) * own + low + side * (8 * own)
+        cols = pl.ds(pl.multiple_of(start, 128), buffer.shape[2])
+        loads.append(pltpu.make_async_copy(x_ref.at[:, cols], buffer.at[d], in_sem.at[d]))
+        loads[d].start()
+    stores = []
+    for i in range(len(loads) // 8):
+        for load in loads[8 * i : 8 * i + 8]:
+            load.wait()
+        rows = pl.ds(8 * i, 8)
+        stores.append(pltpu.make_async_copy(buffer.at[rows], out_ref.at[rows], out_sem.at[i]))
+        stores[i].start()
+    for store in stores:
+        store.wait()
+
+
+def pack(x, own, shift, low, pts):
     count = x.shape[1] // own // 2
-    shapes = [jax.ShapeDtypeStruct((count, x.shape[0], n), x.dtype) for _, _, n in jobs]
-    return pl.pallas_call(
-        functools.partial(pack_kernel, own, [job[:2] for job in jobs]),
-        out_shape=shapes,
+    shape = (count, x.shape[0], pts)
+    return pl.pallas_call(
+        functools.partial(pack_kernel, own, shift, low),
+        out_shape=jax.ShapeDtypeStruct(shape, x.dtype),
         in_specs=[pl.BlockSpec(memory_space=pltpu.HBM)],
-        out_specs=[pl.BlockSpec(memory_space=pltpu.VMEM)] * len(jobs),
-        scratch_shapes=[pltpu.SemaphoreType.DMA((count * len(jobs),))],
+        out_specs=pl.BlockSpec(memory_space=pltpu.HBM),
+        scratch_shapes=[
+            pltpu.VMEM(shape, x.dtype),
+            pltpu.SemaphoreType.DMA((count,)),
+            pltpu.SemaphoreType.DMA((count // 8,)),
+        ],
         compiler_params=pltpu.CompilerParams(vmem_limit_bytes=60 * 2**20),
         name="pack",
     )(x)
@@ -248,7 +255,7 @@
 
 def power_kernel(denominator, t_ref, *refs):
     part_refs, (o_ref, m_ref, out_ref, sem) = refs[:-4], refs[-4:]
-    sums = jnp.sum(t_ref[...], axis=0) / denominator
+    sums = jnp.sum(t_ref[...].astype(F32), axis=0) / denominator
     real_rows = [sums[k : k + 1, :] for k in range(PAIRS + 1)]
     imag_rows = [jnp.zeros_like(real_rows[0])] + [sums[PAIRS + k : PAIRS + k + 1, :] for k in range(1, PAIRS + 1)]
     for k in range(PAIRS + 1, NB):
@@ -320,13 +327,13 @@
 
     later = own - FIRST
     low = later - LAST
-    (first,) = pack(x, own, [(1, later, FIRST)])
+    first = pack(x, own, 1, later, FIRST)
     first = lax.ppermute(first, "zh", swap)
-    (pass_on,) = pack(x, own, [(1, 0, later)])
+    pass_on = pack(x, own, 1, 0, later)
     pass_on = exchange(pass_on, PLANE)
     passed = lax.ppermute(pass_on[:, :, :low], "zh", swap)
     last = lax.ppermute(pass_on[:, :, low:], "zh", swap)
-    (mine,) = pack(x, own, [(0, 0, own)])
+    mine = pack(x, own, 0, 0, own)
     x0 = exchange(mine, PLANE)
     side = lax.axis_index("zh")
     place = jnp.arange(local * count // 2, dtype=jnp.int32)
@@ -340,7 +347,7 @@
     s, g1, part2 = whole(w0, w1, x0, first, s)
     s, t, part1 = rest(w1, last, p1, g0, g1, s, low, lax.axis_size(("y", "x")))
     t = exchange(t, ("y", "x")).sum(axis=0)
-    t = to_all(t, ("zh", "zl", "c"))
+    t = to_all(t.astype(BF16), ("zh", "zl", "c"))
     out = power(t, (part0, part1, part2), float(NB * total))
     shape = (1, NB, 2, NF, own)
     return s.reshape(shape), out.reshape(shape)

time: 174 us -> 172 us (0.989)
  no operation moved by 1% of the time
where the time goes in v2:
time: 172 us; the launch traced here: 171 us
  blocking collectives  58.8 us (34%)
  waiting for transfers between devices  44.3 us (26%)
  starting transfers between devices  36.7 us (21%)
  Pallas kernels  18 us (10%)
  local copies, waits for them, and re-layouts  8.42 us (5%)
  other arithmetic  4.34 us (3%)
    all_to_all x1, blocking collectives, to_all(): return lax.all_to_all(copies, axes, 0, 0, tiled=True)  45.5 us
    all_to_all x3, starting transfers between devices, exchange(): return lax.all_to_all(x, axes, 0, 0, tiled=True)  23.8 us
    all_to_all x3, waiting for transfers between devices, exchange(): return lax.all_to_all(x, axes, 0, 0, tiled=True)  16.6 us
    ppermute x1, waiting for transfers between devices, shards(): first = lax.ppermute(first, 'zh', swap)  14.8 us
    all_to_all x1, blocking collectives, exchange(): return lax.all_to_all(x, axes, 0, 0, tiled=True)  13.4 us
    ppermute x1, waiting for transfers between devices, shards(): last = lax.ppermute(pass_on[:, :, low:], 'zh', swap)  8.27 us
    pallas_call x3, Pallas kernels, pack(): pl.pallas_call(functools.partial(pack_kernel, own, shift, low), out_shape...  7.18 us
    ppermute x1, starting transfers between devices, shards(): first = lax.ppermute(first, 'zh', swap)  7 us
  transfers between devices with their start and end apart: 6, of which 4 were waited for; matrix products, arithmetic and copies ran while one was open for 5% of the time, Pallas kernels for 7%

profile of v2, /device:TPU:1, one launch (start us, length us, event | category | flops | bytes accessed | tf_op | source)
XLA Modules:
  0.0 171.4 jit_solution(16735616006390402403)
XLA Ops:
  0.6 2.3 %pack.4 = bf16[32,16,1280]{2,1,0:T(8,128)(2,1)} custom-call(bf16[16,131072]{1,0:T(8,128)(2,1)} %bitcast.10), custom_call_target="tpu_custom_call" | custom-call | tf_op jit(solution)/shard_map/pack/pallas_call | solution.py:77
  3.0 8.6 %all-to-all-start = ((bf16[32,16,1280]{2,1,0:T(8,128)(2,1)}), bf16[32,16,1280]{2,1,0:T(8,128)(2,1)S(1)}, u32[]{:S(2)}, u32[]{:S(2)}) async-start(bf16[32,16,1280]{2,1,0:T(8,128)(2,1)} %pack.4), calls=%async_computation | async-start | bytes 2621440 | tf_op jit(solution)/shard_map/all_to_all | solution.py:317
  11.6 2.7 %pack.5 = bf16[32,16,2048]{2,1,0:T(8,128)(2,1)} custom-call(bf16[16,131072]{1,0:T(8,128)(2,1)} %bitcast.11), custom_call_target="tpu_custom_call" | custom-call | tf_op jit(solution)/shard_map/pack/pallas_call | solution.py:77
  14.3 16.6 %all-to-all-done = bf16[32,16,1280]{2,1,0:T(8,128)(2,1)S(1)} async-done(((bf16[32,16,1280]{2,1,0:T(8,128)(2,1)}), bf16[32,16,1280]{2,1,0:T(8,128)(2,1)S(1)}, u32[]{:S(2)}, u32[]{:S(2)}) %all-to-all-start) | async-done | bytes 1310752 | tf_op jit(solution)/shard_map/all_to_all | solution.py:317
  30.9 1.1 copy-done.8
  31.9 5.2 %all-to-all-start.1 = ((bf16[32,16,2048]{2,1,0:T(8,128)(2,1)}), bf16[32,16,2048]{2,1,0:T(8,128)(2,1)S(1)}, u32[]{:S(2)}, u32[]{:S(2)}) async-start(bf16[32,16,2048]{2,1,0:T(8,128)(2,1)} %pack.5), calls=%async_computation.1 | async-start | bytes 4194304 | tf_op jit(solution)/shard_map/all_to_all | solution.py:317
  37.1 0.0 copy-start.9
  37.1 0.0 copy-start.10
  37.1 2.1 %pack.3 = bf16[32,16,768]{2,1,0:T(8,128)(2,1)} custom-call(bf16[16,131072]{1,0:T(8,128)(2,1)} %bitcast.12), custom_call_target="tpu_custom_call" | custom-call | tf_op jit(solution)/shard_map/pack/pallas_call | solution.py:77
  39.2 7.0 %collective-permute-start = (bf16[32,16,768]{2,1,0:T(8,128)(2,1)}, bf16[32,16,768]{2,1,0:T(8,128)(2,1)}, u32[]{:S(2)}, u32[]{:S(2)}) collective-permute-start(bf16[32,16,768]{2,1,0:T(8,128)(2,1)} %pack.3), channel_id=1, source_target_pairs={{0,32},{32,0},{1,33},{33,1},{2,34},{34,2},{3,35},{35,3},{4,36},{36... | collective-permute-start | bytes 2359304 | tf_op jit(solution)/shard_map/ppermute | solution.py:331
  46.3 0.1 subtract_select_fusion
  46.3 0.2 fusion.15
  46.5 4.0 %multiply_convert_fusion.1 = (bf16[1,7,32,512]{3,2,1,0:T(8,128)(2,1)S(1)}, bf16[1,7,32,512]{3,2,1,0:T(8,128)(2,1)S(1)}, bf16[1,7,32,512]{3,2,1,0:T(8,128)(2,1)S(1)}, bf16[1,7,32,512]{3,2,1,0:T(8,128)(2,1)S(1)}) fusion(f32[7,512]{1,0:T(8,128)S(1)} %get-tuple-element.34, s32[7,512]{1,0:T(8,128)S(1)} %get-tuple-element.42, s32[32]{0:T(128)S(1)} %copy-done.10, ...), kind=kLoop, calls=%fused_computation.19 | loop fusion | flops 4587520 | bytes 1003648 | tf_op jit(solution)/shard_map/convert
  50.6 2.1 %slice.9 = bf16[32,16,768]{2,1,0:T(8,128)(2,1)} slice(bf16[32,16,1280]{2,1,0:T(8,128)(2,1)} %copy-done.8), slice={[0:32], [0:16], [0:768]} | slice | bytes 1572864 | tf_op jit(solution)/shard_map/slice | solution.py:334
  52.6 0.0 collective-permute-start.2
  52.7 14.8 %collective-permute-done = bf16[32,16,768]{2,1,0:T(8,128)(2,1)} collective-permute-done((bf16[32,16,768]{2,1,0:T(8,128)(2,1)}, bf16[32,16,768]{2,1,0:T(8,128)(2,1)}, u32[]{:S(2)}, u32[]{:S(2)}) %collective-permute-start) | collective-permute-done | bytes 786464 | tf_op jit(solution)/shard_map/ppermute | solution.py:331
  67.5 10.1 %all-to-all-start.2 = ((bf16[32,16,768]{2,1,0:T(8,128)(2,1)}), bf16[32,16,768]{2,1,0:T(8,128)(2,1)}, u32[]{:S(2)}, u32[]{:S(2)}) async-start(bf16[32,16,768]{2,1,0:T(8,128)(2,1)} %collective-permute-done), calls=%async_computation.2 | async-start | bytes 1572864 | tf_op jit(solution)/shard_map/all_to_all | solution.py:317
  77.5 1.9 %slice.8 = bf16[32,16,512]{2,1,0:T(8,128)(2,1)} slice(bf16[32,16,1280]{2,1,0:T(8,128)(2,1)} %copy-done.8), slice={[0:32], [0:16], [768:1280]} | slice | bytes 1048576 | tf_op jit(solution)/shard_map/slice | solution.py:335
  79.4 5.8 %collective-permute-start.1 = (bf16[32,16,512]{2,1,0:T(8,128)(2,1)}, bf16[32,16,512]{2,1,0:T(8,128)(2,1)S(1)}, u32[]{:S(2)}, u32[]{:S(2)}) collective-permute-start(bf16[32,16,512]{2,1,0:T(8,128)(2,1)} %slice.8), channel_id=1, source_target_pairs={{0,32},{32,0},{1,33},{33,1},{2,34},{34,2},{3,35},{35,3},{4,36},{36... | collective-permute-start | bytes 1572872 | tf_op jit(solution)/shard_map/ppermute | solution.py:335
  85.2 0.8 partial.1
  86.0 0.9 copy-done
  86.9 4.7 %collective-permute-done.2.x_ref = bf16[32,16,768]{2,1,0:T(8,128)(2,1)} collective-permute-done((bf16[32,16,768]{2,1,0:T(8,128)(2,1)}, bf16[32,16,768]{2,1,0:T(8,128)(2,1)}, u32[]{:S(2)}, u32[]{:S(2)}) %collective-permute-start.2) | collective-permute-done | bytes 786464 | tf_op jit(solution)/shard_map/ppermute | solution.py:334
  91.6 2.6 %middle.1 = (bf16[448,2048]{1,0:T(8,128)(2,1)}, f32[448,224]{1,0:T(8,128)S(1)}, bf16[448,768]{1,0:T(8,128)(2,1)S(1)}) custom-call(bf16[448,512]{1,0:T(8,128)(2,1)S(1)} %bitcast.5, bf16[32,16,768]{2,1,0:T(8,128)(2,1)} %collective-permute-done.2.x_ref, f32[448,768]{1,0:T(8,128)S(1)} %get-tuple-element.19.p_ref), custom_call_target="tpu_custom_call" | custom-call | flops 352321536 | bytes 4194304 | tf_op jit(solution)/shard_map/middle/pallas_call | solution.py:188
  94.3 0.8 copy-done.2
  95.1 0.8 copy-done.6
  95.9 3.2 %whole.1 = (bf16[448,2048]{1,0:T(8,128)(2,1)}, f32[448,224]{1,0:T(8,128)S(1)}, bf16[448,768]{1,0:T(8,128)(2,1)S(1)}) custom-call(bf16[448,512]{1,0:T(8,128)(2,1)S(1)} %bitcast.9, bf16[448,512]{1,0:T(8,128)(2,1)S(1)} %bitcast.6, bf16[32,16,2048]{2,1,0:T(8,128)(2,1)S(1)} %all-to-all-done.1.x_ref.x0_ref, ...), custom_call_target="tpu_custom_call", output_to_operand_aliasing={{0}: (4, {})} | custom-call | flops 704643072 | bytes 4194304 | tf_op jit(solution)/shard_map/whole/pallas_call | solution.py:125
  99.2 0.8 copy-done.4
  100.0 8.3 %collective-permute-done.1.x_ref = bf16[32,16,512]{2,1,0:T(8,128)(2,1)S(1)} collective-permute-done((bf16[32,16,512]{2,1,0:T(8,128)(2,1)}, bf16[32,16,512]{2,1,0:T(8,128)(2,1)S(1)}, u32[]{:S(2)}, u32[]{:S(2)}) %collective-permute-start.1) | collective-permute-done | bytes 524320 | tf_op jit(solution)/shard_map/ppermute | solution.py:335
  108.3 1.4 rest.1
  109.7 13.4 %all_to_all.25 = f32[16,8,256]{2,1,0:T(8,128)S(1)} all-to-all(f32[16,8,256]{2,1,0:T(8,128)S(1)} %get-tuple-element.26), channel_id=1, replica_groups=mesh['y'=4,'zh'=2,'x'=4,'c'=2,'zl'=4] {'y','x'}, dimensions={0} | all-to-all | bytes 262144 | tf_op jit(solution)/shard_map/all_to_all | solution.py:317
  123.1 45.5 %all_to_all.26.t_ref = bf16[16,8,256]{2,1,0:T(8,128)(2,1)S(1)} all-to-all(bf16[16,8,256]{2,1,0:T(8,128)(2,1)S(1)} %broadcast_in_dim.11), channel_id=1, replica_groups=mesh['y'=4,'zh'=2,'x'=4,'c'=2,'zl'=4] {'zh','zl','c'}, dimensions={0} | all-to-all | bytes 131072 | tf_op jit(solution)/shard_map/all_to_all | solution.py:313
  168.6 2.8 %power.1 = f32[448,2048]{1,0:T(8,128)} custom-call(bf16[16,8,256]{2,1,0:T(8,128)(2,1)S(1)} %all_to_all.26.t_ref, bf16[448,768]{1,0:T(8,128)(2,1)S(1)} %copy-done.3, bf16[448,512]{1,0:T(8,128)(2,1)S(1)} %get-tuple-element.28.refs_1_, bf16[448,768]{1,0:T(8,128)(2,1)S(1)} %copy-done.5), custom_call_target="tpu_custom_call" | custom-call | tf_op jit(solution)/shard_map/power/pallas_call | solution.py:296
  (22 shorter events, 0.2 us)
Async XLA Ops:
  3.0 27.9 %all-to-all-start = ((bf16[32,16,1280]{2,1,0:T(8,128)(2,1)}), bf16[32,16,1280]{2,1,0:T(8,128)(2,1)S(1)}, u32[]{:S(2)}, u32[]{:S(2)}) async-start(bf16[32,16,1280]{2,1,0:T(8,128)(2,1)} %pack.4), calls=%async_computation | async-start | bytes 2621440 | tf_op jit(solution)/shard_map/all_to_all | solution.py:317
  30.9 1.1 copy-start.8
  31.9 35.6 %all-to-all-start.1 = ((bf16[32,16,2048]{2,1,0:T(8,128)(2,1)}), bf16[32,16,2048]{2,1,0:T(8,128)(2,1)S(1)}, u32[]{:S(2)}, u32[]{:S(2)}) async-start(bf16[32,16,2048]{2,1,0:T(8,128)(2,1)} %pack.5), calls=%async_computation.1 | async-start | bytes 4194304 | tf_op jit(solution)/shard_map/all_to_all | solution.py:317
  37.1 9.2 %copy-start.9 = (s32[7]{0:T(128)S(1)}, s32[7]{0:T(128)}, u32[]{:S(2)}) copy-start(s32[7]{0:T(128)} %param.4) | copy-start | bytes 88
  37.1 9.4 %copy-start.10 = (s32[32]{0:T(128)S(1)}, s32[32]{0:T(128)}, u32[]{:S(2)}) copy-start(s32[32]{0:T(128)} %param.5) | copy-start | bytes 388
  39.2 28.2 %collective-permute-start = (bf16[32,16,768]{2,1,0:T(8,128)(2,1)}, bf16[32,16,768]{2,1,0:T(8,128)(2,1)}, u32[]{:S(2)}, u32[]{:S(2)}) collective-permute-start(bf16[32,16,768]{2,1,0:T(8,128)(2,1)} %pack.3), channel_id=1, source_target_pairs={{0,32},{32,0},{1,33},{33,1},{2,34},{34,2},{3,35},{35,3},{4,36},{36... | collective-permute-start | bytes 2359304 | tf_op jit(solution)/shard_map/ppermute | solution.py:331
  52.6 39.0 %collective-permute-start.2 = (bf16[32,16,768]{2,1,0:T(8,128)(2,1)}, bf16[32,16,768]{2,1,0:T(8,128)(2,1)}, u32[]{:S(2)}, u32[]{:S(2)}) collective-permute-start(bf16[32,16,768]{2,1,0:T(8,128)(2,1)} %slice.9), channel_id=1, source_target_pairs={{0,32},{32,0},{1,33},{33,1},{2,34},{34,2},{3,35},{35,3},{4,36},{36... | collective-permute-start | bytes 2359304 | tf_op jit(solution)/shard_map/ppermute | solution.py:334
  67.5 28.4 %all-to-all-start.2 = ((bf16[32,16,768]{2,1,0:T(8,128)(2,1)}), bf16[32,16,768]{2,1,0:T(8,128)(2,1)}, u32[]{:S(2)}, u32[]{:S(2)}) async-start(bf16[32,16,768]{2,1,0:T(8,128)(2,1)} %collective-permute-done), calls=%async_computation.2 | async-start | bytes 1572864 | tf_op jit(solution)/shard_map/all_to_all | solution.py:317
  79.4 28.9 %collective-permute-start.1 = (bf16[32,16,512]{2,1,0:T(8,128)(2,1)}, bf16[32,16,512]{2,1,0:T(8,128)(2,1)S(1)}, u32[]{:S(2)}, u32[]{:S(2)}) collective-permute-start(bf16[32,16,512]{2,1,0:T(8,128)(2,1)} %slice.8), channel_id=1, source_target_pairs={{0,32},{32,0},{1,33},{33,1},{2,34},{34,2},{3,35},{35,3},{4,36},{36... | collective-permute-start | bytes 1572872 | tf_op jit(solution)/shard_map/ppermute | solution.py:335
  86.0 0.9 copy-start
  94.3 0.8 copy-start.2
  95.1 0.8 copy-start.6
  95.9 12.4 %copy-start.1 = (f32[448,512]{1,0:T(8,128)S(1)}, f32[448,512]{1,0:T(8,128)}, u32[]{:S(2)}) copy-start(f32[448,512]{1,0:T(8,128)} %copy-done) | copy-start | bytes 2752516
  95.9 12.4 %copy-start.7 = (f32[448,224]{1,0:T(8,128)S(1)}, f32[448,224]{1,0:T(8,128)}, u32[]{:S(2)}) copy-start(f32[448,224]{1,0:T(8,128)} %copy-done.6) | copy-start | bytes 1204228
  99.1 0.9 copy-start.4
  108.3 60.3 %copy-start.3 = (bf16[448,768]{1,0:T(8,128)(2,1)S(1)}, bf16[448,768]{1,0:T(8,128)(2,1)}, u32[]{:S(2)}) copy-start(bf16[448,768]{1,0:T(8,128)(2,1)} %copy-done.2) | copy-start | bytes 2064388
  108.3 60.3 %copy-start.5 = (bf16[448,768]{1,0:T(8,128)(2,1)S(1)}, bf16[448,768]{1,0:T(8,128)(2,1)}, u32[]{:S(2)}) copy-start(bf16[448,768]{1,0:T(8,128)(2,1)} %copy-done.4) | copy-start | bytes 2064388

commit v3 on v2

--- a/solution.py
+++ b/solution.py
@@ -19,7 +19,7 @@
 TA = ("y", "zh", "x", "c")
 PLANE = ("y", "x", "c")
 FIRST = 768
-LAST = 512
+LAST = 256
 F32 = jnp.float32
 BF16 = jnp.bfloat16
 
@@ -253,7 +253,7 @@
     return (col == row // NF * 2 * NF + part * NF + row % NF).astype(BF16)
 
 
-def power_kernel(denominator, t_ref, *refs):
+def power_kernel(denominator, lows, t_ref, *refs):
     part_refs, (o_ref, m_ref, out_ref, sem) = refs[:-4], refs[-4:]
     sums = jnp.sum(t_ref[...].astype(F32), axis=0) / denominator
     real_rows = [sums[k : k + 1, :] for k in range(PAIRS + 1)]
@@ -277,8 +277,7 @@
             row = jnp.broadcast_to(table[b : b + 1], (NF, ROWS))
             m_ref[at : at + NF, :] = jnp.where(same, row, 0.0).astype(BF16)
     stores = []
-    low = 0
-    for part_ref in part_refs:
+    for low, part_ref in zip(lows, part_refs):
         for at in range(0, part_ref.shape[1], 512):
             values = part_ref[:, at : at + 512]
             cols = pl.ds(low, values.shape[1])
@@ -290,11 +289,11 @@
         store.wait()
 
 
-def power(t, parts, denominator):
+def power(t, parts, lows, denominator):
     pts = sum(part.shape[1] for part in parts)
     here = pl.BlockSpec(memory_space=pltpu.VMEM)
     return pl.pallas_call(
-        functools.partial(power_kernel, denominator),
+        functools.partial(power_kernel, denominator, lows),
         out_shape=jax.ShapeDtypeStruct((ROWS, pts), F32),
         in_specs=[here] * (1 + len(parts)),
         out_specs=pl.BlockSpec(memory_space=pl.ANY),
@@ -348,7 +347,7 @@
     s, t, part1 = rest(w1, last, p1, g0, g1, s, low, lax.axis_size(("y", "x")))
     t = exchange(t, ("y", "x")).sum(axis=0)
     t = to_all(t.astype(BF16), ("zh", "zl", "c"))
-    out = power(t, (part0, part1, part2), float(NB * total))
+    out = power(t, (part1, part0, part2), (low, 0, later), float(NB * total))
     shape = (1, NB, 2, NF, own)
     return s.reshape(shape), out.reshape(shape)
 

time: 172 us -> 177 us (1.029)
  blocking collectives: 58.8 us -> 62.8 us
    ppermute x1, waiting for transfers between devices: 4.71 us -> 13.2 us  [shards(): passed = lax.ppermute(pass_on[:, :, :low], 'zh', swap)]
    ppermute x1, waiting for transfers between devices: 8.27 us -> 0.65 us  [shards(): last = lax.ppermute(pass_on[:, :, low:], 'zh', swap)]
    all_to_all x1, blocking collectives: 45.5 us -> 49.4 us  [to_all(): return lax.all_to_all(copies, axes, 0, 0, tiled=True)]
    unnamed x22 -> x18, local copies, waits for them, and re-layouts: 4.47 us -> 3.65 us
where the time goes in v3:
time: 177 us; the launch traced here: 176 us
  blocking collectives  62.8 us (35%)
  waiting for transfers between devices  45 us (25%)
  starting transfers between devices  36.7 us (21%)
  Pallas kernels  19 us (11%)
  local copies, waits for them, and re-layouts  7.66 us (4%)
  other arithmetic  4.33 us (2%)
    all_to_all x1, blocking collectives, to_all(): return lax.all_to_all(copies, axes, 0, 0, tiled=True)  49.4 us
    all_to_all x3, starting transfers between devices, exchange(): return lax.all_to_all(x, axes, 0, 0, tiled=True)  23.8 us
    all_to_all x3, waiting for transfers between devices, exchange(): return lax.all_to_all(x, axes, 0, 0, tiled=True)  16.6 us
    ppermute x1, waiting for transfers between devices, shards(): first = lax.ppermute(first, 'zh', swap)  14.5 us
    all_to_all x1, blocking collectives, exchange(): return lax.all_to_all(x, axes, 0, 0, tiled=True)  13.4 us
    ppermute x1, waiting for transfers between devices, shards(): passed = lax.ppermute(pass_on[:, :, :low], 'zh', swap)  13.2 us
    pallas_call x3, Pallas kernels, pack(): pl.pallas_call(functools.partial(pack_kernel, own, shift, low), out_shape...  7.16 us
    ppermute x1, starting transfers between devices, shards(): first = lax.ppermute(first, 'zh', swap)  7 us
  transfers between devices with their start and end apart: 6, of which 4 were waited for; matrix products, arithmetic and copies ran while one was open for 5% of the time, Pallas kernels for 7%

profile of v3, /device:TPU:1, one launch (start us, length us, event | category | flops | bytes accessed | tf_op | source)
XLA Modules:
  0.0 176.2 jit_solution(17633704688152002940)
XLA Ops:
  0.6 2.3 %pack.4 = bf16[32,16,1280]{2,1,0:T(8,128)(2,1)} custom-call(bf16[16,131072]{1,0:T(8,128)(2,1)} %bitcast.10), custom_call_target="tpu_custom_call" | custom-call | tf_op jit(solution)/shard_map/pack/pallas_call | solution.py:77
  3.0 8.6 %all-to-all-start = ((bf16[32,16,1280]{2,1,0:T(8,128)(2,1)}), bf16[32,16,1280]{2,1,0:T(8,128)(2,1)S(1)}, u32[]{:S(2)}, u32[]{:S(2)}) async-start(bf16[32,16,1280]{2,1,0:T(8,128)(2,1)} %pack.4), calls=%async_computation | async-start | bytes 2621440 | tf_op jit(solution)/shard_map/all_to_all | solution.py:316
  11.6 2.7 %pack.5 = bf16[32,16,2048]{2,1,0:T(8,128)(2,1)} custom-call(bf16[16,131072]{1,0:T(8,128)(2,1)} %bitcast.11), custom_call_target="tpu_custom_call" | custom-call | tf_op jit(solution)/shard_map/pack/pallas_call | solution.py:77
  14.3 16.6 %all-to-all-done = bf16[32,16,1280]{2,1,0:T(8,128)(2,1)S(1)} async-done(((bf16[32,16,1280]{2,1,0:T(8,128)(2,1)}), bf16[32,16,1280]{2,1,0:T(8,128)(2,1)S(1)}, u32[]{:S(2)}, u32[]{:S(2)}) %all-to-all-start) | async-done | bytes 1310752 | tf_op jit(solution)/shard_map/all_to_all | solution.py:316
  30.9 1.1 copy-done.6
  31.9 5.2 %all-to-all-start.1 = ((bf16[32,16,2048]{2,1,0:T(8,128)(2,1)}), bf16[32,16,2048]{2,1,0:T(8,128)(2,1)S(1)}, u32[]{:S(2)}, u32[]{:S(2)}) async-start(bf16[32,16,2048]{2,1,0:T(8,128)(2,1)} %pack.5), calls=%async_computation.1 | async-start | bytes 4194304 | tf_op jit(solution)/shard_map/all_to_all | solution.py:316
  37.1 0.0 copy-start.7
  37.1 2.1 %pack.3 = bf16[32,16,768]{2,1,0:T(8,128)(2,1)} custom-call(bf16[16,131072]{1,0:T(8,128)(2,1)} %bitcast.12), custom_call_target="tpu_custom_call" | custom-call | tf_op jit(solution)/shard_map/pack/pallas_call | solution.py:77
  39.2 0.0 copy-start.8
  39.2 7.0 %collective-permute-start = (bf16[32,16,768]{2,1,0:T(8,128)(2,1)}, bf16[32,16,768]{2,1,0:T(8,128)(2,1)}, u32[]{:S(2)}, u32[]{:S(2)}) collective-permute-start(bf16[32,16,768]{2,1,0:T(8,128)(2,1)} %pack.3), channel_id=1, source_target_pairs={{0,32},{32,0},{1,33},{33,1},{2,34},{34,2},{3,35},{35,3},{4,36},{36... | collective-permute-start | bytes 2359304 | tf_op jit(solution)/shard_map/ppermute | solution.py:330
  46.2 0.1 subtract_select_fusion
  46.3 0.2 fusion.15
  46.5 2.3 %slice.9 = bf16[32,16,1024]{2,1,0:T(8,128)(2,1)} slice(bf16[32,16,1280]{2,1,0:T(8,128)(2,1)} %copy-done.6), slice={[0:32], [0:16], [0:1024]} | slice | bytes 2097152 | tf_op jit(solution)/shard_map/slice | solution.py:333
  48.8 0.0 collective-permute-start.2
  48.9 3.9 %multiply_convert_fusion.1 = (bf16[1,7,32,512]{3,2,1,0:T(8,128)(2,1)S(1)}, bf16[1,7,32,512]{3,2,1,0:T(8,128)(2,1)S(1)}, bf16[1,7,32,512]{3,2,1,0:T(8,128)(2,1)S(1)}, bf16[1,7,32,512]{3,2,1,0:T(8,128)(2,1)S(1)}) fusion(f32[7,512]{1,0:T(8,128)S(1)} %get-tuple-element.34, s32[7,512]{1,0:T(8,128)S(1)} %get-tuple-element.42, s32[32]{0:T(128)S(1)} %copy-done.8, ...), kind=kLoop, calls=%fused_computation.19 | loop fusion | flops 4587520 | bytes 1003648 | tf_op jit(solution)/shard_map/convert
  52.9 14.5 %collective-permute-done = bf16[32,16,768]{2,1,0:T(8,128)(2,1)} collective-permute-done((bf16[32,16,768]{2,1,0:T(8,128)(2,1)}, bf16[32,16,768]{2,1,0:T(8,128)(2,1)}, u32[]{:S(2)}, u32[]{:S(2)}) %collective-permute-start) | collective-permute-done | bytes 786464 | tf_op jit(solution)/shard_map/ppermute | solution.py:330
  67.5 10.1 %all-to-all-start.2 = ((bf16[32,16,768]{2,1,0:T(8,128)(2,1)}), bf16[32,16,768]{2,1,0:T(8,128)(2,1)}, u32[]{:S(2)}, u32[]{:S(2)}) async-start(bf16[32,16,768]{2,1,0:T(8,128)(2,1)} %collective-permute-done), calls=%async_computation.2 | async-start | bytes 1572864 | tf_op jit(solution)/shard_map/all_to_all | solution.py:316
  77.5 1.7 slice.8
  79.2 5.8 %collective-permute-start.1 = (bf16[32,16,256]{2,1,0:T(8,128)(2,1)}, bf16[32,16,256]{2,1,0:T(8,128)(2,1)}, u32[]{:S(2)}, u32[]{:S(2)}) collective-permute-start(bf16[32,16,256]{2,1,0:T(8,128)(2,1)} %slice.8), channel_id=1, source_target_pairs={{0,32},{32,0},{1,33},{33,1},{2,34},{34,2},{3,35},{35,3},{4,36},{36... | collective-permute-start | bytes 786440 | tf_op jit(solution)/shard_map/ppermute | solution.py:334
  85.0 0.8 partial.1
  85.8 13.2 %collective-permute-done.2.x_ref = bf16[32,16,1024]{2,1,0:T(8,128)(2,1)} collective-permute-done((bf16[32,16,1024]{2,1,0:T(8,128)(2,1)}, bf16[32,16,1024]{2,1,0:T(8,128)(2,1)}, u32[]{:S(2)}, u32[]{:S(2)}) %collective-permute-start.2) | collective-permute-done | bytes 1048608 | tf_op jit(solution)/shard_map/ppermute | solution.py:333
  99.0 2.9 %middle.1 = (bf16[448,2048]{1,0:T(8,128)(2,1)}, f32[448,224]{1,0:T(8,128)S(1)}, bf16[448,1024]{1,0:T(8,128)(2,1)S(1)}) custom-call(bf16[448,512]{1,0:T(8,128)(2,1)S(1)} %bitcast.5, bf16[32,16,1024]{2,1,0:T(8,128)(2,1)} %collective-permute-done.2.x_ref, f32[448,1024]{1,0:T(8,128)S(1)} %get-tuple-element.19.p_ref), custom_call_target="tpu_custom_call" | custom-call | flops 469762048 | bytes 4194304 | tf_op jit(solution)/shard_map/middle/pallas_call | solution.py:188
  101.9 0.0 copy-start
  102.0 0.9 copy-done
  102.9 0.8 copy-done.4
  103.7 3.2 %whole.1 = (bf16[448,2048]{1,0:T(8,128)(2,1)}, f32[448,224]{1,0:T(8,128)S(1)}, bf16[448,768]{1,0:T(8,128)(2,1)S(1)}) custom-call(bf16[448,512]{1,0:T(8,128)(2,1)S(1)} %bitcast.9, bf16[448,512]{1,0:T(8,128)(2,1)S(1)} %bitcast.6, bf16[32,16,2048]{2,1,0:T(8,128)(2,1)S(1)} %all-to-all-done.1.x_ref.x0_ref, ...), custom_call_target="tpu_custom_call", output_to_operand_aliasing={{0}: (4, {})} | custom-call | flops 704643072 | bytes 4194304 | tf_op jit(solution)/shard_map/whole/pallas_call | solution.py:125
  106.8 0.9 copy-done.2
  107.7 0.7 collective-permute-done.1.x_ref
  108.4 2.2 %rest.1 = (bf16[448,2048]{1,0:T(8,128)(2,1)}, f32[16,8,256]{2,1,0:T(8,128)S(1)}, bf16[448,256]{1,0:T(8,128)(2,1)S(1)}) custom-call(bf16[448,512]{1,0:T(8,128)(2,1)S(1)} %bitcast.7, bf16[32,16,256]{2,1,0:T(8,128)(2,1)} %collective-permute-done.1.x_ref, f32[448,256]{1,0:T(8,128)S(1)} %get-tuple-element.18.p_ref, ...), custom_call_target="tpu_custom_call", output_to_operand_aliasing={{0}: (5, {})} | custom-call | flops 117440512 | bytes 4194304 | tf_op jit(solution)/shard_map/rest/pallas_call | solution.py:233
  110.5 13.4 %all_to_all.25 = f32[16,8,256]{2,1,0:T(8,128)S(1)} all-to-all(f32[16,8,256]{2,1,0:T(8,128)S(1)} %get-tuple-element.26), channel_id=1, replica_groups=mesh['y'=4,'zh'=2,'x'=4,'c'=2,'zl'=4] {'y','x'}, dimensions={0} | all-to-all | bytes 262144 | tf_op jit(solution)/shard_map/all_to_all | solution.py:316
  123.9 49.4 %all_to_all.26.t_ref = bf16[16,8,256]{2,1,0:T(8,128)(2,1)S(1)} all-to-all(bf16[16,8,256]{2,1,0:T(8,128)(2,1)S(1)} %broadcast_in_dim.11), channel_id=1, replica_groups=mesh['y'=4,'zh'=2,'x'=4,'c'=2,'zl'=4] {'zh','zl','c'}, dimensions={0} | all-to-all | bytes 131072 | tf_op jit(solution)/shard_map/all_to_all | solution.py:312
  173.3 2.9 %power.1 = f32[448,2048]{1,0:T(8,128)} custom-call(bf16[16,8,256]{2,1,0:T(8,128)(2,1)S(1)} %all_to_all.26.t_ref, bf16[448,256]{1,0:T(8,128)(2,1)S(1)} %get-tuple-element.27.refs_0_, bf16[448,1024]{1,0:T(8,128)(2,1)S(1)} %copy-done.1, bf16[448,768]{1,0:T(8,128)(2,1)S(1)} %copy-done.3), custom_call_target="tpu_custom_call" | custom-call | tf_op jit(solution)/shard_map/power/pallas_call | solution.py:295
  (18 shorter events, 0.1 us)
Async XLA Ops:
  3.0 27.9 %all-to-all-start = ((bf16[32,16,1280]{2,1,0:T(8,128)(2,1)}), bf16[32,16,1280]{2,1,0:T(8,128)(2,1)S(1)}, u32[]{:S(2)}, u32[]{:S(2)}) async-start(bf16[32,16,1280]{2,1,0:T(8,128)(2,1)} %pack.4), calls=%async_computation | async-start | bytes 2621440 | tf_op jit(solution)/shard_map/all_to_all | solution.py:316
  30.9 1.1 copy-start.6
  31.9 35.5 %all-to-all-start.1 = ((bf16[32,16,2048]{2,1,0:T(8,128)(2,1)}), bf16[32,16,2048]{2,1,0:T(8,128)(2,1)S(1)}, u32[]{:S(2)}, u32[]{:S(2)}) async-start(bf16[32,16,2048]{2,1,0:T(8,128)(2,1)} %pack.5), calls=%async_computation.1 | async-start | bytes 4194304 | tf_op jit(solution)/shard_map/all_to_all | solution.py:316
  37.1 9.1 %copy-start.7 = (s32[7]{0:T(128)S(1)}, s32[7]{0:T(128)}, u32[]{:S(2)}) copy-start(s32[7]{0:T(128)} %param.4) | copy-start | bytes 88
  39.2 9.7 %copy-start.8 = (s32[32]{0:T(128)S(1)}, s32[32]{0:T(128)}, u32[]{:S(2)}) copy-start(s32[32]{0:T(128)} %param.5) | copy-start | bytes 388
  39.2 28.2 %collective-permute-start = (bf16[32,16,768]{2,1,0:T(8,128)(2,1)}, bf16[32,16,768]{2,1,0:T(8,128)(2,1)}, u32[]{:S(2)}, u32[]{:S(2)}) collective-permute-start(bf16[32,16,768]{2,1,0:T(8,128)(2,1)} %pack.3), channel_id=1, source_target_pairs={{0,32},{32,0},{1,33},{33,1},{2,34},{34,2},{3,35},{35,3},{4,36},{36... | collective-permute-start | bytes 2359304 | tf_op jit(solution)/shard_map/ppermute | solution.py:330
  48.8 50.2 %collective-permute-start.2 = (bf16[32,16,1024]{2,1,0:T(8,128)(2,1)}, bf16[32,16,1024]{2,1,0:T(8,128)(2,1)}, u32[]{:S(2)}, u32[]{:S(2)}) collective-permute-start(bf16[32,16,1024]{2,1,0:T(8,128)(2,1)} %slice.9), channel_id=1, source_target_pairs={{0,32},{32,0},{1,33},{33,1},{2,34},{34,2},{3,35},{35,3},{4,36},{36... | collective-permute-start | bytes 3145736 | tf_op jit(solution)/shard_map/ppermute | solution.py:333
  67.5 36.2 %all-to-all-start.2 = ((bf16[32,16,768]{2,1,0:T(8,128)(2,1)}), bf16[32,16,768]{2,1,0:T(8,128)(2,1)}, u32[]{:S(2)}, u32[]{:S(2)}) async-start(bf16[32,16,768]{2,1,0:T(8,128)(2,1)} %collective-permute-done), calls=%async_computation.2 | async-start | bytes 1572864 | tf_op jit(solution)/shard_map/all_to_all | solution.py:316
  79.2 29.2 %collective-permute-start.1 = (bf16[32,16,256]{2,1,0:T(8,128)(2,1)}, bf16[32,16,256]{2,1,0:T(8,128)(2,1)}, u32[]{:S(2)}, u32[]{:S(2)}) collective-permute-start(bf16[32,16,256]{2,1,0:T(8,128)(2,1)} %slice.8), channel_id=1, source_target_pairs={{0,32},{32,0},{1,33},{33,1},{2,34},{34,2},{3,35},{35,3},{4,36},{36... | collective-permute-start | bytes 786440 | tf_op jit(solution)/shard_map/ppermute | solution.py:334
  101.9 0.9 copy-start
  102.9 0.8 copy-start.4
  103.7 4.7 %copy-start.5 = (f32[448,224]{1,0:T(8,128)S(1)}, f32[448,224]{1,0:T(8,128)}, u32[]{:S(2)}) copy-start(f32[448,224]{1,0:T(8,128)} %copy-done.4) | copy-start | bytes 1204228
  106.8 0.9 copy-start.2
  108.4 65.0 %copy-start.1 = (bf16[448,1024]{1,0:T(8,128)(2,1)S(1)}, bf16[448,1024]{1,0:T(8,128)(2,1)}, u32[]{:S(2)}) copy-start(bf16[448,1024]{1,0:T(8,128)(2,1)} %copy-done) | copy-start | bytes 2752516
  108.4 65.0 %copy-start.3 = (bf16[448,768]{1,0:T(8,128)(2,1)S(1)}, bf16[448,768]{1,0:T(8,128)(2,1)}, u32[]{:S(2)}) copy-start(bf16[448,768]{1,0:T(8,128)(2,1)} %copy-done.2) | copy-start | bytes 2064388

commit v4 on v2

--- a/solution.py
+++ b/solution.py
@@ -327,7 +327,9 @@
 
     later = own - FIRST
     low = later - LAST
-    first = pack(x, own, 1, later, FIRST)
+    tiles = x.reshape(local // 8, 8, 4, 2, 8, own).transpose(0, 2, 3, 4, 1, 5)
+    far = 1 - lax.axis_index("zh")
+    first = lax.dynamic_slice(tiles, (0, 0, far, 0, 0, later), (local // 8, 4, 1, 8, 8, FIRST))
     first = lax.ppermute(first, "zh", swap)
     pass_on = pack(x, own, 1, 0, later)
     pass_on = exchange(pass_on, PLANE)
@@ -341,7 +343,8 @@
     w0 = weights(block_starts, kept_freqs, times + side * 128)
     w1 = weights(block_starts, kept_freqs, times + (1 - side) * 128)
     first, w0, w1 = lax.optimization_barrier((first, w0, w1))
-    first = exchange(first, PLANE)
+    first = first.reshape(local // 8, count // 2, 8, FIRST).transpose(1, 0, 2, 3)
+    first = exchange(first.reshape(count // 2, local, FIRST), PLANE)
     p0, p1 = partial(w0, x0, (low, LAST))
     s, g0, part0 = middle(w1, passed, p0, own)
     s, g1, part2 = whole(w0, w1, x0, first, s)

time: 172 us -> 173 us (level)
  local copies, waits for them, and re-layouts: 8.42 us -> 11.5 us
  Pallas kernels: 18 us -> 15.9 us
    pallas_call x3 -> x2, Pallas kernels: 7.18 us -> 5.06 us  [pack(): pl.pallas_call(functools.partial(pack_kernel, own, shift, low), out_shape...]
    ppermute x1, waiting for transfers between devices: 4.71 us -> 2.62 us  [shards(): passed = lax.ppermute(pass_on[:, :, :low], 'zh', swap)]
    dynamic_slice x0 -> x1, local copies, waits for them, and re-layouts: none -> 2.09 us  [shards(): lax.dynamic_slice(tiles, (0, 0, far, 0, 0, later), (local // 8, 4, 1, 8,...]
    optimization_barrier x0 -> x1, local copies, waits for them, and re-layouts: none -> 2.08 us  [shards(): first, w0, w1 = lax.optimization_barrier((first, w0, w1))]
    unnamed x22 -> x24, local copies, waits for them, and re-layouts: 4.47 us -> 4.47 us
  transfers between devices with their start and end apart: 6 -> 6, of which waited for: 4 -> 4; matrix products, arithmetic and copies ran while one was open for 5% -> 7% of each run, Pallas kernels for 7% -> 5%
where the time goes in v4:
time: 173 us; the launch traced here: 172 us
  blocking collectives  60 us (35%)
  waiting for transfers between devices  43.3 us (25%)
  starting transfers between devices  36.6 us (21%)
  Pallas kernels  15.9 us (9%)
  local copies, waits for them, and re-layouts  11.5 us (7%)
  other arithmetic  4.35 us (3%)
    all_to_all x1, blocking collectives, to_all(): return lax.all_to_all(copies, axes, 0, 0, tiled=True)  46.6 us
    all_to_all x3, starting transfers between devices, exchange(): return lax.all_to_all(x, axes, 0, 0, tiled=True)  23.8 us
    all_to_all x3, waiting for transfers between devices, exchange(): return lax.all_to_all(x, axes, 0, 0, tiled=True)  16.5 us
    ppermute x1, waiting for transfers between devices, shards(): first = lax.ppermute(first, 'zh', swap)  15.9 us
    all_to_all x1, blocking collectives, exchange(): return lax.all_to_all(x, axes, 0, 0, tiled=True)  13.4 us
    ppermute x1, waiting for transfers between devices, shards(): last = lax.ppermute(pass_on[:, :, low:], 'zh', swap)  8.28 us
    ppermute x1, starting transfers between devices, shards(): first = lax.ppermute(first, 'zh', swap)  6.91 us
    ppermute x1, starting transfers between devices, shards(): last = lax.ppermute(pass_on[:, :, low:], 'zh', swap)  5.82 us
  transfers between devices with their start and end apart: 6, of which 4 were waited for; matrix products, arithmetic and copies ran while one was open for 7% of the time, Pallas kernels for 5%

profile of v4, /device:TPU:1, one launch (start us, length us, event | category | flops | bytes accessed | tf_op | source)
XLA Modules:
  0.0 172.4 jit_solution(13996474221250420895)
XLA Ops:
  0.6 2.3 %pack.2 = bf16[32,16,1280]{2,1,0:T(8,128)(2,1)} custom-call(bf16[16,131072]{1,0:T(8,128)(2,1)} %bitcast.18), custom_call_target="tpu_custom_call" | custom-call | tf_op jit(solution)/shard_map/pack/pallas_call | solution.py:77
  3.0 8.6 %all-to-all-start = ((bf16[32,16,1280]{2,1,0:T(8,128)(2,1)}), bf16[32,16,1280]{2,1,0:T(8,128)(2,1)S(1)}, u32[]{:S(2)}, u32[]{:S(2)}) async-start(bf16[32,16,1280]{2,1,0:T(8,128)(2,1)} %pack.2), calls=%async_computation | async-start | bytes 2621440 | tf_op jit(solution)/shard_map/all_to_all | solution.py:317
  11.6 2.7 %pack.3 = bf16[32,16,2048]{2,1,0:T(8,128)(2,1)} custom-call(bf16[16,131072]{1,0:T(8,128)(2,1)} %bitcast.19), custom_call_target="tpu_custom_call" | custom-call | tf_op jit(solution)/shard_map/pack/pallas_call | solution.py:77
  14.3 0.0 copy-start.10
  14.3 16.5 %all-to-all-done = bf16[32,16,1280]{2,1,0:T(8,128)(2,1)S(1)} async-done(((bf16[32,16,1280]{2,1,0:T(8,128)(2,1)}), bf16[32,16,1280]{2,1,0:T(8,128)(2,1)S(1)}, u32[]{:S(2)}, u32[]{:S(2)}) %all-to-all-start) | async-done | bytes 1310752 | tf_op jit(solution)/shard_map/all_to_all | solution.py:317
  30.9 1.1 copy-done.8
  31.9 5.2 %all-to-all-start.1 = ((bf16[32,16,2048]{2,1,0:T(8,128)(2,1)}), bf16[32,16,2048]{2,1,0:T(8,128)(2,1)S(1)}, u32[]{:S(2)}, u32[]{:S(2)}) async-start(bf16[32,16,2048]{2,1,0:T(8,128)(2,1)} %pack.3), calls=%async_computation.1 | async-start | bytes 4194304 | tf_op jit(solution)/shard_map/all_to_all | solution.py:317
  37.1 2.1 %dynamic-slice_bitcast_fusion = bf16[2,4,1,8,8,768]{5,4,3,2,1,0:T(8,128)(2,1)} fusion(bf16[2,8,4,2,8,2048]{5,1,4,3,2,0:T(8,128)(2,1)} %bitcast.20, s32[]{:T(128)S(6)} %select_n.101), kind=kLoop, calls=%fused_computation.6 | loop fusion | bytes 1572868 | tf_op jit(solution)/shard_map/dynamic_slice | solution.py:332
  39.2 6.9 %collective-permute-start = (bf16[2,4,1,8,8,768]{5,4,3,2,1,0:T(8,128)(2,1)}, bf16[2,4,1,8,8,768]{5,4,3,2,1,0:T(8,128)(2,1)}, u32[]{:S(2)}, u32[]{:S(2)}) collective-permute-start(bf16[2,4,1,8,8,768]{5,4,3,2,1,0:T(8,128)(2,1)} %dynamic-slice_bitcast_fusion), channel_id=1, source_target_pairs={{0,32},{32,0},{1,33},{33,1},{2,34},{34,2},{3,35},{35,3},{4,36},{36... | collective-permute-start | bytes 2359304 | tf_op jit(solution)/shard_map/ppermute | solution.py:333
  46.1 0.1 subtract_select_fusion
  46.2 0.2 fusion.15
  46.4 4.0 %multiply_convert_fusion.1 = (bf16[1,7,32,512]{3,2,1,0:T(8,128)(2,1)S(1)}, bf16[1,7,32,512]{3,2,1,0:T(8,128)(2,1)S(1)}, bf16[1,7,32,512]{3,2,1,0:T(8,128)(2,1)S(1)}, bf16[1,7,32,512]{3,2,1,0:T(8,128)(2,1)S(1)}) fusion(f32[7,512]{1,0:T(8,128)S(1)} %get-tuple-element.34, s32[7,512]{1,0:T(8,128)S(1)} %get-tuple-element.42, s32[32]{0:T(128)S(1)} %copy-done.11, ...), kind=kLoop, calls=%fused_computation.20 | loop fusion | flops 4587520 | bytes 1003648 | tf_op jit(solution)/shard_map/convert
  50.4 0.9 slice.9
  51.4 0.0 collective-permute-start.2
  51.4 15.9 %collective-permute-done = bf16[2,4,1,8,8,768]{5,4,3,2,1,0:T(8,128)(2,1)} collective-permute-done((bf16[2,4,1,8,8,768]{5,4,3,2,1,0:T(8,128)(2,1)}, bf16[2,4,1,8,8,768]{5,4,3,2,1,0:T(8,128)(2,1)}, u32[]{:S(2)}, u32[]{:S(2)}) %collective-permute-start) | collective-permute-done | bytes 786464 | tf_op jit(solution)/shard_map/ppermute | solution.py:333
  67.3 2.1 %copy.7 = bf16[2,4,1,8,8,768]{5,4,0,3,1,2:T(8,128)(2,1)} copy(bf16[2,4,1,8,8,768]{5,4,3,2,1,0:T(8,128)(2,1)} %collective-permute-done) | data formatting | bytes 1572864 | tf_op jit(solution)/shard_map/optimization_barrier | solution.py:345
  69.4 10.1 %all-to-all-start.2 = ((bf16[32,16,768]{2,1,0:T(8,128)(2,1)}), bf16[32,16,768]{2,1,0:T(8,128)(2,1)}, u32[]{:S(2)}, u32[]{:S(2)}) async-start(bf16[32,16,768]{2,1,0:T(8,128)(2,1)} %bitcast.23), calls=%async_computation.2 | async-start | bytes 1572864 | tf_op jit(solution)/shard_map/all_to_all | solution.py:317
  79.5 1.9 %slice.8 = bf16[32,16,512]{2,1,0:T(8,128)(2,1)} slice(bf16[32,16,1280]{2,1,0:T(8,128)(2,1)} %copy-done.8), slice={[0:32], [0:16], [768:1280]} | slice | bytes 1048576 | tf_op jit(solution)/shard_map/slice | solution.py:337
  81.4 5.8 %collective-permute-start.1 = (bf16[32,16,512]{2,1,0:T(8,128)(2,1)}, bf16[32,16,512]{2,1,0:T(8,128)(2,1)S(1)}, u32[]{:S(2)}, u32[]{:S(2)}) collective-permute-start(bf16[32,16,512]{2,1,0:T(8,128)(2,1)} %slice.8), channel_id=1, source_target_pairs={{0,32},{32,0},{1,33},{33,1},{2,34},{34,2},{3,35},{35,3},{4,36},{36... | collective-permute-start | bytes 1572872 | tf_op jit(solution)/shard_map/ppermute | solution.py:337
  87.2 0.8 partial.1
  88.0 0.9 copy-done
  88.9 2.6 %collective-permute-done.2.x_ref = bf16[32,16,768]{2,1,0:T(8,128)(2,1)} collective-permute-done((bf16[32,16,768]{2,1,0:T(8,128)(2,1)}, bf16[32,16,768]{2,1,0:T(8,128)(2,1)}, u32[]{:S(2)}, u32[]{:S(2)}) %collective-permute-start.2) | collective-permute-done | bytes 786464 | tf_op jit(solution)/shard_map/ppermute | solution.py:336
  91.5 2.6 %middle.1 = (bf16[448,2048]{1,0:T(8,128)(2,1)}, f32[448,224]{1,0:T(8,128)S(1)}, bf16[448,768]{1,0:T(8,128)(2,1)S(1)}) custom-call(bf16[448,512]{1,0:T(8,128)(2,1)S(1)} %bitcast.13, bf16[32,16,768]{2,1,0:T(8,128)(2,1)} %collective-permute-done.2.x_ref, f32[448,768]{1,0:T(8,128)S(1)} %get-tuple-element.19.p_ref), custom_call_target="tpu_custom_call" | custom-call | flops 352321536 | bytes 4194304 | tf_op jit(solution)/shard_map/middle/pallas_call | solution.py:188
  94.1 0.8 copy-done.2
  95.0 0.8 copy-done.6
  95.8 3.2 %whole.1 = (bf16[448,2048]{1,0:T(8,128)(2,1)}, f32[448,224]{1,0:T(8,128)S(1)}, bf16[448,768]{1,0:T(8,128)(2,1)S(1)}) custom-call(bf16[448,512]{1,0:T(8,128)(2,1)S(1)} %bitcast.17, bf16[448,512]{1,0:T(8,128)(2,1)S(1)} %bitcast.14, bf16[32,16,2048]{2,1,0:T(8,128)(2,1)S(1)} %all-to-all-done.1.x_ref.x0_ref, ...), custom_call_target="tpu_custom_call", output_to_operand_aliasing={{0}: (4, {})} | custom-call | flops 704643072 | bytes 4194304 | tf_op jit(solution)/shard_map/whole/pallas_call | solution.py:125
  99.0 0.8 copy-done.4
  99.8 8.3 %collective-permute-done.1.x_ref = bf16[32,16,512]{2,1,0:T(8,128)(2,1)S(1)} collective-permute-done((bf16[32,16,512]{2,1,0:T(8,128)(2,1)}, bf16[32,16,512]{2,1,0:T(8,128)(2,1)S(1)}, u32[]{:S(2)}, u32[]{:S(2)}) %collective-permute-start.1) | collective-permute-done | bytes 524320 | tf_op jit(solution)/shard_map/ppermute | solution.py:337
  108.1 1.4 rest.1
  109.6 13.4 %all_to_all.25 = f32[16,8,256]{2,1,0:T(8,128)S(1)} all-to-all(f32[16,8,256]{2,1,0:T(8,128)S(1)} %get-tuple-element.26), channel_id=1, replica_groups=mesh['y'=4,'zh'=2,'x'=4,'c'=2,'zl'=4] {'y','x'}, dimensions={0} | all-to-all | bytes 262144 | tf_op jit(solution)/shard_map/all_to_all | solution.py:317
  123.0 46.6 %all_to_all.26.t_ref = bf16[16,8,256]{2,1,0:T(8,128)(2,1)S(1)} all-to-all(bf16[16,8,256]{2,1,0:T(8,128)(2,1)S(1)} %broadcast_in_dim.11), channel_id=1, replica_groups=mesh['y'=4,'zh'=2,'x'=4,'c'=2,'zl'=4] {'zh','zl','c'}, dimensions={0} | all-to-all | bytes 131072 | tf_op jit(solution)/shard_map/all_to_all | solution.py:313
  169.6 2.8 %power.1 = f32[448,2048]{1,0:T(8,128)} custom-call(bf16[16,8,256]{2,1,0:T(8,128)(2,1)S(1)} %all_to_all.26.t_ref, bf16[448,768]{1,0:T(8,128)(2,1)S(1)} %copy-done.3, bf16[448,512]{1,0:T(8,128)(2,1)S(1)} %get-tuple-element.28.refs_1_, bf16[448,768]{1,0:T(8,128)(2,1)S(1)} %copy-done.5), custom_call_target="tpu_custom_call" | custom-call | tf_op jit(solution)/shard_map/power/pallas_call | solution.py:296
  (25 shorter events, 0.2 us)
Async XLA Ops:
  3.0 27.9 %all-to-all-start = ((bf16[32,16,1280]{2,1,0:T(8,128)(2,1)}), bf16[32,16,1280]{2,1,0:T(8,128)(2,1)S(1)}, u32[]{:S(2)}, u32[]{:S(2)}) async-start(bf16[32,16,1280]{2,1,0:T(8,128)(2,1)} %pack.2), calls=%async_computation | async-start | bytes 2621440 | tf_op jit(solution)/shard_map/all_to_all | solution.py:317
  14.3 31.8 %copy-start.10 = (s32[7]{0:T(128)S(1)}, s32[7]{0:T(128)}, u32[]{:S(2)}) copy-start(s32[7]{0:T(128)} %param.4) | copy-start | bytes 88
  14.3 32.1 %copy-start.11 = (s32[32]{0:T(128)S(1)}, s32[32]{0:T(128)}, u32[]{:S(2)}) copy-start(s32[32]{0:T(128)} %param.5) | copy-start | bytes 388
  30.9 1.1 copy-start.8
  31.9 37.5 %all-to-all-start.1 = ((bf16[32,16,2048]{2,1,0:T(8,128)(2,1)}), bf16[32,16,2048]{2,1,0:T(8,128)(2,1)S(1)}, u32[]{:S(2)}, u32[]{:S(2)}) async-start(bf16[32,16,2048]{2,1,0:T(8,128)(2,1)} %pack.3), calls=%async_computation.1 | async-start | bytes 4194304 | tf_op jit(solution)/shard_map/all_to_all | solution.py:317
  39.2 28.1 %collective-permute-start = (bf16[2,4,1,8,8,768]{5,4,3,2,1,0:T(8,128)(2,1)}, bf16[2,4,1,8,8,768]{5,4,3,2,1,0:T(8,128)(2,1)}, u32[]{:S(2)}, u32[]{:S(2)}) collective-permute-start(bf16[2,4,1,8,8,768]{5,4,3,2,1,0:T(8,128)(2,1)} %dynamic-slice_bitcast_fusion), channel_id=1, source_target_pairs={{0,32},{32,0},{1,33},{33,1},{2,34},{34,2},{3,35},{35,3},{4,36},{36... | collective-permute-start | bytes 2359304 | tf_op jit(solution)/shard_map/ppermute | solution.py:333
  46.1 4.3 %copy-start.9 = (bf16[32,16,1280]{2,1,0:T(8,128)(2,1)S(1)}, bf16[32,16,1280]{2,1,0:T(8,128)(2,1)}, u32[]{:S(2)}) copy-start(bf16[32,16,1280]{2,1,0:T(8,128)(2,1)} %copy-done.8) | copy-start | bytes 3932164
  51.4 40.1 %collective-permute-start.2 = (bf16[32,16,768]{2,1,0:T(8,128)(2,1)}, bf16[32,16,768]{2,1,0:T(8,128)(2,1)}, u32[]{:S(2)}, u32[]{:S(2)}) collective-permute-start(bf16[32,16,768]{2,1,0:T(8,128)(2,1)} %slice.9), channel_id=1, source_target_pairs={{0,32},{32,0},{1,33},{33,1},{2,34},{34,2},{3,35},{35,3},{4,36},{36... | collective-permute-start | bytes 2359304 | tf_op jit(solution)/shard_map/ppermute | solution.py:336
  69.4 26.4 %all-to-all-start.2 = ((bf16[32,16,768]{2,1,0:T(8,128)(2,1)}), bf16[32,16,768]{2,1,0:T(8,128)(2,1)}, u32[]{:S(2)}, u32[]{:S(2)}) async-start(bf16[32,16,768]{2,1,0:T(8,128)(2,1)} %bitcast.23), calls=%async_computation.2 | async-start | bytes 1572864 | tf_op jit(solution)/shard_map/all_to_all | solution.py:317
  81.4 26.8 %collective-permute-start.1 = (bf16[32,16,512]{2,1,0:T(8,128)(2,1)}, bf16[32,16,512]{2,1,0:T(8,128)(2,1)S(1)}, u32[]{:S(2)}, u32[]{:S(2)}) collective-permute-start(bf16[32,16,512]{2,1,0:T(8,128)(2,1)} %slice.8), channel_id=1, source_target_pairs={{0,32},{32,0},{1,33},{33,1},{2,34},{34,2},{3,35},{35,3},{4,36},{36... | collective-permute-start | bytes 1572872 | tf_op jit(solution)/shard_map/ppermute | solution.py:337
  87.9 0.9 copy-start
  94.1 0.8 copy-start.2
  95.0 0.8 copy-start.6
  95.8 12.4 %copy-start.1 = (f32[448,512]{1,0:T(8,128)S(1)}, f32[448,512]{1,0:T(8,128)}, u32[]{:S(2)}) copy-start(f32[448,512]{1,0:T(8,128)} %copy-done) | copy-start | bytes 2752516
  95.8 12.4 %copy-start.7 = (f32[448,224]{1,0:T(8,128)S(1)}, f32[448,224]{1,0:T(8,128)}, u32[]{:S(2)}) copy-start(f32[448,224]{1,0:T(8,128)} %copy-done.6) | copy-start | bytes 1204228
  99.0 0.9 copy-start.4
  108.1 61.4 %copy-start.3 = (bf16[448,768]{1,0:T(8,128)(2,1)S(1)}, bf16[448,768]{1,0:T(8,128)(2,1)}, u32[]{:S(2)}) copy-start(bf16[448,768]{1,0:T(8,128)(2,1)} %copy-done.2) | copy-start | bytes 2064388
  108.1 61.4 %copy-start.5 = (bf16[448,768]{1,0:T(8,128)(2,1)S(1)}, bf16[448,768]{1,0:T(8,128)(2,1)}, u32[]{:S(2)}) copy-start(bf16[448,768]{1,0:T(8,128)(2,1)} %copy-done.4) | copy-start | bytes 2064388

commit v5 on v2

--- a/solution.py
+++ b/solution.py
@@ -220,6 +220,7 @@
     rows = [row_ref[k : k + 1, :] for k in range(2 * NB)]
     imag = [rows[NB + k] - turned(rows[2 * NB - k], k) for k in range(1, PAIRS + 1)]
     sums = jnp.concatenate(rows[: PAIRS + 1] + imag + [jnp.zeros_like(imag[0])], axis=0)
+    sums = sums.astype(BF16)
     for i in range(t_ref.shape[0]):
         t_ref[i] = sums
     save.wait()
@@ -234,7 +235,7 @@
         functools.partial(rest_kernel, low),
         out_shape=(
             jax.ShapeDtypeStruct(s.shape, BF16),
-            jax.ShapeDtypeStruct((copies, 8, 256), F32),
+            jax.ShapeDtypeStruct((copies, 8, 256), BF16),
             jax.ShapeDtypeStruct((ROWS, width), BF16),
         ),
         in_specs=[here] * 5 + [there],
@@ -265,11 +266,11 @@
     tables = []
     for rows in (real_rows, imag_rows):
         picked = [sum(jnp.where((block + k) % NB == b, rows[k][:, :HALF], 0.0) for k in range(NB)) for b in range(NB)]
-        tables.append(jnp.concatenate(picked, axis=0).astype(BF16))
-    real, imag = tables
-    spread = [spread_to(part) for part in range(2)]
-    from_real = dot(real, spread[0]) - dot(imag, spread[1])
-    from_imag = dot(imag, spread[0]) + dot(real, spread[1])
+        tables += picked
+    both = jnp.concatenate(tables, axis=0).astype(BF16)
+    near, far = dot(both, spread_to(0)), dot(both, spread_to(1))
+    from_real = near[:NB] - far[NB:]
+    from_imag = near[NB:] + far[:NB]
     same = lax.broadcasted_iota(jnp.int32, (NF, ROWS), 0) == lax.broadcasted_iota(jnp.int32, (NF, ROWS), 1) % NF
     for b in range(NB):
         for part, table in enumerate((from_real, from_imag)):
@@ -279,8 +280,10 @@
     stores = []
     low = 0
     for part_ref in part_refs:
-        for at in range(0, part_ref.shape[1], 512):
-            values = part_ref[:, at : at + 512]
+        count = part_ref.shape[1]
+        edges = sorted({0, count % 512, *range(count % 512, count + 1, 512)})
+        for at, end in zip(edges, edges[1:]):
+            values = part_ref[:, at:end]
             cols = pl.ds(low, values.shape[1])
             out_ref[:, low : low + values.shape[1]] = dot(m_ref[...], values)
             stores.append(pltpu.make_async_copy(out_ref.at[:, cols], o_ref.at[:, cols], sem.at[len(stores)]))
@@ -346,7 +349,7 @@
     s, g0, part0 = middle(w1, passed, p0, own)
     s, g1, part2 = whole(w0, w1, x0, first, s)
     s, t, part1 = rest(w1, last, p1, g0, g1, s, low, lax.axis_size(("y", "x")))
-    t = exchange(t, ("y", "x")).sum(axis=0)
+    t = exchange(t, ("y", "x")).astype(F32).sum(axis=0)
     t = to_all(t.astype(BF16), ("zh", "zl", "c"))
     out = power(t, (part0, part1, part2), float(NB * total))
     shape = (1, NB, 2, NF, own)

time: 172 us -> 172 us (level)
  no operation moved by 1% of the time
where the time goes in v5:
time: 172 us; the launch traced here: 171 us
  blocking collectives  58.5 us (34%)
  waiting for transfers between devices  44.3 us (26%)
  starting transfers between devices  36.7 us (21%)
  Pallas kernels  17.8 us (10%)
  local copies, waits for them, and re-layouts  8.42 us (5%)
  other arithmetic  4.35 us (3%)
    all_to_all x1, blocking collectives, to_all(): return lax.all_to_all(copies, axes, 0, 0, tiled=True)  45.5 us
    all_to_all x3, starting transfers between devices, exchange(): return lax.all_to_all(x, axes, 0, 0, tiled=True)  23.8 us
    all_to_all x3, waiting for transfers between devices, exchange(): return lax.all_to_all(x, axes, 0, 0, tiled=True)  16.6 us
    ppermute x1, waiting for transfers between devices, shards(): first = lax.ppermute(first, 'zh', swap)  14.8 us
    all_to_all x1, blocking collectives, exchange(): return lax.all_to_all(x, axes, 0, 0, tiled=True)  13.1 us
    ppermute x1, waiting for transfers between devices, shards(): last = lax.ppermute(pass_on[:, :, low:], 'zh', swap)  8.27 us
    pallas_call x3, Pallas kernels, pack(): pl.pallas_call(functools.partial(pack_kernel, own, shift, low), out_shape...  7.18 us
    ppermute x1, starting transfers between devices, shards(): first = lax.ppermute(first, 'zh', swap)  7 us
  transfers between devices with their start and end apart: 6, of which 4 were waited for; matrix products, arithmetic and copies ran while one was open for 5% of the time, Pallas kernels for 7%

profile of v5, /device:TPU:1, one launch (start us, length us, event | category | flops | bytes accessed | tf_op | source)
XLA Modules:
  0.0 170.9 jit_solution(16936064529212285678)
XLA Ops:
  0.6 2.3 %pack.4 = bf16[32,16,1280]{2,1,0:T(8,128)(2,1)} custom-call(bf16[16,131072]{1,0:T(8,128)(2,1)} %bitcast.10), custom_call_target="tpu_custom_call" | custom-call | tf_op jit(solution)/shard_map/pack/pallas_call | solution.py:77
  3.0 8.6 %all-to-all-start = ((bf16[32,16,1280]{2,1,0:T(8,128)(2,1)}), bf16[32,16,1280]{2,1,0:T(8,128)(2,1)S(1)}, u32[]{:S(2)}, u32[]{:S(2)}) async-start(bf16[32,16,1280]{2,1,0:T(8,128)(2,1)} %pack.4), calls=%async_computation | async-start | bytes 2621440 | tf_op jit(solution)/shard_map/all_to_all | solution.py:320
  11.6 2.7 %pack.5 = bf16[32,16,2048]{2,1,0:T(8,128)(2,1)} custom-call(bf16[16,131072]{1,0:T(8,128)(2,1)} %bitcast.11), custom_call_target="tpu_custom_call" | custom-call | tf_op jit(solution)/shard_map/pack/pallas_call | solution.py:77
  14.3 16.6 %all-to-all-done = bf16[32,16,1280]{2,1,0:T(8,128)(2,1)S(1)} async-done(((bf16[32,16,1280]{2,1,0:T(8,128)(2,1)}), bf16[32,16,1280]{2,1,0:T(8,128)(2,1)S(1)}, u32[]{:S(2)}, u32[]{:S(2)}) %all-to-all-start) | async-done | bytes 1310752 | tf_op jit(solution)/shard_map/all_to_all | solution.py:320
  30.9 1.1 copy-done.8
  31.9 5.2 %all-to-all-start.1 = ((bf16[32,16,2048]{2,1,0:T(8,128)(2,1)}), bf16[32,16,2048]{2,1,0:T(8,128)(2,1)S(1)}, u32[]{:S(2)}, u32[]{:S(2)}) async-start(bf16[32,16,2048]{2,1,0:T(8,128)(2,1)} %pack.5), calls=%async_computation.1 | async-start | bytes 4194304 | tf_op jit(solution)/shard_map/all_to_all | solution.py:320
  37.1 0.0 copy-start.9
  37.1 0.0 copy-start.10
  37.1 2.1 %pack.3 = bf16[32,16,768]{2,1,0:T(8,128)(2,1)} custom-call(bf16[16,131072]{1,0:T(8,128)(2,1)} %bitcast.12), custom_call_target="tpu_custom_call" | custom-call | tf_op jit(solution)/shard_map/pack/pallas_call | solution.py:77
  39.2 7.0 %collective-permute-start = (bf16[32,16,768]{2,1,0:T(8,128)(2,1)}, bf16[32,16,768]{2,1,0:T(8,128)(2,1)}, u32[]{:S(2)}, u32[]{:S(2)}) collective-permute-start(bf16[32,16,768]{2,1,0:T(8,128)(2,1)} %pack.3), channel_id=1, source_target_pairs={{0,32},{32,0},{1,33},{33,1},{2,34},{34,2},{3,35},{35,3},{4,36},{36... | collective-permute-start | bytes 2359304 | tf_op jit(solution)/shard_map/ppermute | solution.py:334
  46.3 0.1 subtract_select_fusion
  46.3 0.2 fusion.15
  46.5 4.0 %multiply_convert_fusion.1 = (bf16[1,7,32,512]{3,2,1,0:T(8,128)(2,1)S(1)}, bf16[1,7,32,512]{3,2,1,0:T(8,128)(2,1)S(1)}, bf16[1,7,32,512]{3,2,1,0:T(8,128)(2,1)S(1)}, bf16[1,7,32,512]{3,2,1,0:T(8,128)(2,1)S(1)}) fusion(f32[7,512]{1,0:T(8,128)S(1)} %get-tuple-element.34, s32[7,512]{1,0:T(8,128)S(1)} %get-tuple-element.42, s32[32]{0:T(128)S(1)} %copy-done.10, ...), kind=kLoop, calls=%fused_computation.19 | loop fusion | flops 4587520 | bytes 1003648 | tf_op jit(solution)/shard_map/convert.1
  50.6 2.1 %slice.9 = bf16[32,16,768]{2,1,0:T(8,128)(2,1)} slice(bf16[32,16,1280]{2,1,0:T(8,128)(2,1)} %copy-done.8), slice={[0:32], [0:16], [0:768]} | slice | bytes 1572864 | tf_op jit(solution)/shard_map/slice | solution.py:337
  52.6 0.0 collective-permute-start.2
  52.7 14.8 %collective-permute-done = bf16[32,16,768]{2,1,0:T(8,128)(2,1)} collective-permute-done((bf16[32,16,768]{2,1,0:T(8,128)(2,1)}, bf16[32,16,768]{2,1,0:T(8,128)(2,1)}, u32[]{:S(2)}, u32[]{:S(2)}) %collective-permute-start) | collective-permute-done | bytes 786464 | tf_op jit(solution)/shard_map/ppermute | solution.py:334
  67.5 10.1 %all-to-all-start.2 = ((bf16[32,16,768]{2,1,0:T(8,128)(2,1)}), bf16[32,16,768]{2,1,0:T(8,128)(2,1)}, u32[]{:S(2)}, u32[]{:S(2)}) async-start(bf16[32,16,768]{2,1,0:T(8,128)(2,1)} %collective-permute-done), calls=%async_computation.2 | async-start | bytes 1572864 | tf_op jit(solution)/shard_map/all_to_all | solution.py:320
  77.5 1.9 %slice.8 = bf16[32,16,512]{2,1,0:T(8,128)(2,1)} slice(bf16[32,16,1280]{2,1,0:T(8,128)(2,1)} %copy-done.8), slice={[0:32], [0:16], [768:1280]} | slice | bytes 1048576 | tf_op jit(solution)/shard_map/slice | solution.py:338
  79.4 5.8 %collective-permute-start.1 = (bf16[32,16,512]{2,1,0:T(8,128)(2,1)}, bf16[32,16,512]{2,1,0:T(8,128)(2,1)S(1)}, u32[]{:S(2)}, u32[]{:S(2)}) collective-permute-start(bf16[32,16,512]{2,1,0:T(8,128)(2,1)} %slice.8), channel_id=1, source_target_pairs={{0,32},{32,0},{1,33},{33,1},{2,34},{34,2},{3,35},{35,3},{4,36},{36... | collective-permute-start | bytes 1572872 | tf_op jit(solution)/shard_map/ppermute | solution.py:338
  85.2 0.8 partial.1
  86.0 0.9 copy-done
  86.9 4.7 %collective-permute-done.2.x_ref = bf16[32,16,768]{2,1,0:T(8,128)(2,1)} collective-permute-done((bf16[32,16,768]{2,1,0:T(8,128)(2,1)}, bf16[32,16,768]{2,1,0:T(8,128)(2,1)}, u32[]{:S(2)}, u32[]{:S(2)}) %collective-permute-start.2) | collective-permute-done | bytes 786464 | tf_op jit(solution)/shard_map/ppermute | solution.py:337
  91.6 2.6 %middle.1 = (bf16[448,2048]{1,0:T(8,128)(2,1)}, f32[448,224]{1,0:T(8,128)S(1)}, bf16[448,768]{1,0:T(8,128)(2,1)S(1)}) custom-call(bf16[448,512]{1,0:T(8,128)(2,1)S(1)} %bitcast.5, bf16[32,16,768]{2,1,0:T(8,128)(2,1)} %collective-permute-done.2.x_ref, f32[448,768]{1,0:T(8,128)S(1)} %get-tuple-element.19.p_ref), custom_call_target="tpu_custom_call" | custom-call | flops 352321536 | bytes 4194304 | tf_op jit(solution)/shard_map/middle/pallas_call | solution.py:188
  94.3 0.8 copy-done.2
  95.1 0.8 copy-done.6
  95.9 3.2 %whole.1 = (bf16[448,2048]{1,0:T(8,128)(2,1)}, f32[448,224]{1,0:T(8,128)S(1)}, bf16[448,768]{1,0:T(8,128)(2,1)S(1)}) custom-call(bf16[448,512]{1,0:T(8,128)(2,1)S(1)} %bitcast.9, bf16[448,512]{1,0:T(8,128)(2,1)S(1)} %bitcast.6, bf16[32,16,2048]{2,1,0:T(8,128)(2,1)S(1)} %all-to-all-done.1.x_ref.x0_ref, ...), custom_call_target="tpu_custom_call", output_to_operand_aliasing={{0}: (4, {})} | custom-call | flops 704643072 | bytes 4194304 | tf_op jit(solution)/shard_map/whole/pallas_call | solution.py:125
  99.2 0.8 copy-done.4
  100.0 8.3 %collective-permute-done.1.x_ref = bf16[32,16,512]{2,1,0:T(8,128)(2,1)S(1)} collective-permute-done((bf16[32,16,512]{2,1,0:T(8,128)(2,1)}, bf16[32,16,512]{2,1,0:T(8,128)(2,1)S(1)}, u32[]{:S(2)}, u32[]{:S(2)}) %collective-permute-start.1) | collective-permute-done | bytes 524320 | tf_op jit(solution)/shard_map/ppermute | solution.py:338
  108.3 1.3 rest.1
  109.5 13.1 %all_to_all.25 = bf16[16,8,256]{2,1,0:T(8,128)(2,1)S(1)} all-to-all(bf16[16,8,256]{2,1,0:T(8,128)(2,1)S(1)} %get-tuple-element.26), channel_id=1, replica_groups=mesh['y'=4,'zh'=2,'x'=4,'c'=2,'zl'=4] {'y','x'}, dimensions={0} | all-to-all | bytes 131072 | tf_op jit(solution)/shard_map/all_to_all | solution.py:320
  122.6 45.5 %all_to_all.26.t_ref = bf16[16,8,256]{2,1,0:T(8,128)(2,1)S(1)} all-to-all(bf16[16,8,256]{2,1,0:T(8,128)(2,1)S(1)} %broadcast_in_dim.11), channel_id=1, replica_groups=mesh['y'=4,'zh'=2,'x'=4,'c'=2,'zl'=4] {'zh','zl','c'}, dimensions={0} | all-to-all | bytes 131072 | tf_op jit(solution)/shard_map/all_to_all | solution.py:316
  168.1 2.8 %power.1 = f32[448,2048]{1,0:T(8,128)} custom-call(bf16[16,8,256]{2,1,0:T(8,128)(2,1)S(1)} %all_to_all.26.t_ref, bf16[448,768]{1,0:T(8,128)(2,1)S(1)} %copy-done.3, bf16[448,512]{1,0:T(8,128)(2,1)S(1)} %get-tuple-element.28.refs_1_, bf16[448,768]{1,0:T(8,128)(2,1)S(1)} %copy-done.5), custom_call_target="tpu_custom_call" | custom-call | tf_op jit(solution)/shard_map/power/pallas_call | solution.py:299
  (22 shorter events, 0.2 us)
Async XLA Ops:
  3.0 27.9 %all-to-all-start = ((bf16[32,16,1280]{2,1,0:T(8,128)(2,1)}), bf16[32,16,1280]{2,1,0:T(8,128)(2,1)S(1)}, u32[]{:S(2)}, u32[]{:S(2)}) async-start(bf16[32,16,1280]{2,1,0:T(8,128)(2,1)} %pack.4), calls=%async_computation | async-start | bytes 2621440 | tf_op jit(solution)/shard_map/all_to_all | solution.py:320
  30.9 1.1 copy-start.8
  31.9 35.6 %all-to-all-start.1 = ((bf16[32,16,2048]{2,1,0:T(8,128)(2,1)}), bf16[32,16,2048]{2,1,0:T(8,128)(2,1)S(1)}, u32[]{:S(2)}, u32[]{:S(2)}) async-start(bf16[32,16,2048]{2,1,0:T(8,128)(2,1)} %pack.5), calls=%async_computation.1 | async-start | bytes 4194304 | tf_op jit(solution)/shard_map/all_to_all | solution.py:320
  37.1 9.2 %copy-start.9 = (s32[7]{0:T(128)S(1)}, s32[7]{0:T(128)}, u32[]{:S(2)}) copy-start(s32[7]{0:T(128)} %param.4) | copy-start | bytes 88
  37.1 9.4 %copy-start.10 = (s32[32]{0:T(128)S(1)}, s32[32]{0:T(128)}, u32[]{:S(2)}) copy-start(s32[32]{0:T(128)} %param.5) | copy-start | bytes 388
  39.2 28.2 %collective-permute-start = (bf16[32,16,768]{2,1,0:T(8,128)(2,1)}, bf16[32,16,768]{2,1,0:T(8,128)(2,1)}, u32[]{:S(2)}, u32[]{:S(2)}) collective-permute-start(bf16[32,16,768]{2,1,0:T(8,128)(2,1)} %pack.3), channel_id=1, source_target_pairs={{0,32},{32,0},{1,33},{33,1},{2,34},{34,2},{3,35},{35,3},{4,36},{36... | collective-permute-start | bytes 2359304 | tf_op jit(solution)/shard_map/ppermute | solution.py:334
  52.6 39.0 %collective-permute-start.2 = (bf16[32,16,768]{2,1,0:T(8,128)(2,1)}, bf16[32,16,768]{2,1,0:T(8,128)(2,1)}, u32[]{:S(2)}, u32[]{:S(2)}) collective-permute-start(bf16[32,16,768]{2,1,0:T(8,128)(2,1)} %slice.9), channel_id=1, source_target_pairs={{0,32},{32,0},{1,33},{33,1},{2,34},{34,2},{3,35},{35,3},{4,36},{36... | collective-permute-start | bytes 2359304 | tf_op jit(solution)/shard_map/ppermute | solution.py:337
  67.5 28.4 %all-to-all-start.2 = ((bf16[32,16,768]{2,1,0:T(8,128)(2,1)}), bf16[32,16,768]{2,1,0:T(8,128)(2,1)}, u32[]{:S(2)}, u32[]{:S(2)}) async-start(bf16[32,16,768]{2,1,0:T(8,128)(2,1)} %collective-permute-done), calls=%async_computation.2 | async-start | bytes 1572864 | tf_op jit(solution)/shard_map/all_to_all | solution.py:320
  79.4 28.9 %collective-permute-start.1 = (bf16[32,16,512]{2,1,0:T(8,128)(2,1)}, bf16[32,16,512]{2,1,0:T(8,128)(2,1)S(1)}, u32[]{:S(2)}, u32[]{:S(2)}) collective-permute-start(bf16[32,16,512]{2,1,0:T(8,128)(2,1)} %slice.8), channel_id=1, source_target_pairs={{0,32},{32,0},{1,33},{33,1},{2,34},{34,2},{3,35},{35,3},{4,36},{36... | collective-permute-start | bytes 1572872 | tf_op jit(solution)/shard_map/ppermute | solution.py:338
  86.0 0.9 copy-start
  94.3 0.8 copy-start.2
  95.1 0.8 copy-start.6
  95.9 12.4 %copy-start.1 = (f32[448,512]{1,0:T(8,128)S(1)}, f32[448,512]{1,0:T(8,128)}, u32[]{:S(2)}) copy-start(f32[448,512]{1,0:T(8,128)} %copy-done) | copy-start | bytes 2752516
  95.9 12.4 %copy-start.7 = (f32[448,224]{1,0:T(8,128)S(1)}, f32[448,224]{1,0:T(8,128)}, u32[]{:S(2)}) copy-start(f32[448,224]{1,0:T(8,128)} %copy-done.6) | copy-start | bytes 1204228
  99.1 0.9 copy-start.4
  108.3 59.8 %copy-start.3 = (bf16[448,768]{1,0:T(8,128)(2,1)S(1)}, bf16[448,768]{1,0:T(8,128)(2,1)}, u32[]{:S(2)}) copy-start(bf16[448,768]{1,0:T(8,128)(2,1)} %copy-done.2) | copy-start | bytes 2064388
  108.3 59.8 %copy-start.5 = (bf16[448,768]{1,0:T(8,128)(2,1)S(1)}, bf16[448,768]{1,0:T(8,128)(2,1)}, u32[]{:S(2)}) copy-start(bf16[448,768]{1,0:T(8,128)(2,1)} %copy-done.4) | copy-start | bytes 2064388

commit v6 on v5

--- a/solution.py
+++ b/solution.py
@@ -52,41 +52,43 @@
     return row % NF == col % NF
 
 
-def pack_kernel(own, shift, low, x_ref, out_ref, buffer, in_sem, out_sem):
+def pack_kernel(shift, low, x_ref, out_ref, buffer, in_sem, out_sem):
     side = (lax.axis_index("zh") + shift) % 2
+    runs, _, halves, _, pts = buffer.shape
     loads = []
-    for d in range(buffer.shape[0]):
-        start = ((d // 8) * 16 + d % 8) * own + low + side * (8 * own)
-        cols = pl.ds(pl.multiple_of(start, 128), buffer.shape[2])
-        loads.append(pltpu.make_async_copy(x_ref.at[:, cols], buffer.at[d], in_sem.at[d]))
-        loads[d].start()
+    for y in range(runs):
+        for half in range(halves):
+            source = x_ref.at[half, y, side, :, :, pl.ds(low, pts)]
+            loads.append(pltpu.make_async_copy(source, buffer.at[y, :, half], in_sem.at[y * halves + half]))
+            loads[-1].start()
     stores = []
-    for i in range(len(loads) // 8):
-        for load in loads[8 * i : 8 * i + 8]:
+    for y in range(runs):
+        for load in loads[y * halves : (y + 1) * halves]:
             load.wait()
-        rows = pl.ds(8 * i, 8)
-        stores.append(pltpu.make_async_copy(buffer.at[rows], out_ref.at[rows], out_sem.at[i]))
-        stores[i].start()
+        stores.append(pltpu.make_async_copy(buffer.at[y], out_ref.at[y], out_sem.at[y]))
+        stores[y].start()
     for store in stores:
         store.wait()
 
 
 def pack(x, own, shift, low, pts):
-    count = x.shape[1] // own // 2
-    shape = (count, x.shape[0], pts)
-    return pl.pallas_call(
-        functools.partial(pack_kernel, own, shift, low),
+    local = x.shape[0]
+    tiles = x.reshape(local // 8, 8, 4, 2, 8, own).transpose(0, 2, 3, 4, 1, 5)
+    shape = (4, 8, local // 8, 8, pts)
+    packed = pl.pallas_call(
+        functools.partial(pack_kernel, shift, low),
         out_shape=jax.ShapeDtypeStruct(shape, x.dtype),
         in_specs=[pl.BlockSpec(memory_space=pltpu.HBM)],
         out_specs=pl.BlockSpec(memory_space=pltpu.HBM),
         scratch_shapes=[
             pltpu.VMEM(shape, x.dtype),
-            pltpu.SemaphoreType.DMA((count,)),
-            pltpu.SemaphoreType.DMA((count // 8,)),
+            pltpu.SemaphoreType.DMA((4 * (local // 8),)),
+            pltpu.SemaphoreType.DMA((4,)),
         ],
         compiler_params=pltpu.CompilerParams(vmem_limit_bytes=60 * 2**20),
         name="pack",
-    )(x)
+    )(tiles)
+    return packed.reshape(32, local, pts)
 
 
 def emit(parts, s_ref):

time: 172 us -> 171 us (level)
  transfers between devices with their start and end apart: 6 -> 6, of which waited for: 4 -> 4; matrix products, arithmetic and copies ran while one was open for 5% -> 5% of each run, Pallas kernels for 7% -> 6%
where the time goes in v6:
time: 171 us
  blocking collectives  58.5 us (34%)
  waiting for transfers between devices  44.6 us (26%)
  starting transfers between devices  36.7 us (21%)
  Pallas kernels  17.3 us (10%)
  local copies, waits for them, and re-layouts  8.42 us (5%)
  other arithmetic  4.35 us (3%)
    all_to_all x1, blocking collectives, to_all(): return lax.all_to_all(copies, axes, 0, 0, tiled=True)  45.5 us
    all_to_all x3, starting transfers between devices, exchange(): return lax.all_to_all(x, axes, 0, 0, tiled=True)  23.8 us
    all_to_all x3, waiting for transfers between devices, exchange(): return lax.all_to_all(x, axes, 0, 0, tiled=True)  16.8 us
    ppermute x1, waiting for transfers between devices, shards(): first = lax.ppermute(first, 'zh', swap)  14.8 us
    all_to_all x1, blocking collectives, exchange(): return lax.all_to_all(x, axes, 0, 0, tiled=True)  13.1 us
    ppermute x1, waiting for transfers between devices, shards(): last = lax.ppermute(pass_on[:, :, low:], 'zh', swap)  8.27 us
    ppermute x1, starting transfers between devices, shards(): first = lax.ppermute(first, 'zh', swap)  7 us
    pallas_call x3, Pallas kernels, pack(): pl.pallas_call(functools.partial(pack_kernel, shift, low), out_shape=jax....  6.69 us
  transfers between devices with their start and end apart: 6, of which 4 were waited for; matrix products, arithmetic and copies ran while one was open for 5% of the time, Pallas kernels for 6%

profile of v6, /device:TPU:1, one launch (start us, length us, event | category | flops | bytes accessed | tf_op | source)
XLA Modules:
  0.0 170.7 jit_solution(9206955810093026788)
XLA Ops:
  0.6 2.2 %pack.4 = bf16[4,8,2,8,1280]{4,3,2,1,0:T(8,128)(2,1)} custom-call(bf16[2,4,2,8,8,2048]{5,4,3,2,1,0:T(8,128)(2,1)} %bitcast.15), custom_call_target="tpu_custom_call" | custom-call | tf_op jit(solution)/shard_map/pack/pallas_call | solution.py:78
  2.9 8.6 %all-to-all-start = ((bf16[32,16,1280]{2,1,0:T(8,128)(2,1)}), bf16[32,16,1280]{2,1,0:T(8,128)(2,1)S(1)}, u32[]{:S(2)}, u32[]{:S(2)}) async-start(bf16[32,16,1280]{2,1,0:T(8,128)(2,1)} %bitcast.20), calls=%async_computation | async-start | bytes 2621440 | tf_op jit(solution)/shard_map/all_to_all | solution.py:322
  11.5 2.5 %pack.5 = bf16[4,8,2,8,2048]{4,3,2,1,0:T(8,128)(2,1)} custom-call(bf16[2,4,2,8,8,2048]{5,4,3,2,1,0:T(8,128)(2,1)} %bitcast.16), custom_call_target="tpu_custom_call" | custom-call | tf_op jit(solution)/shard_map/pack/pallas_call | solution.py:78
  13.9 16.8 %all-to-all-done = bf16[32,16,1280]{2,1,0:T(8,128)(2,1)S(1)} async-done(((bf16[32,16,1280]{2,1,0:T(8,128)(2,1)}), bf16[32,16,1280]{2,1,0:T(8,128)(2,1)S(1)}, u32[]{:S(2)}, u32[]{:S(2)}) %all-to-all-start) | async-done | bytes 1310752 | tf_op jit(solution)/shard_map/all_to_all | solution.py:322
  30.7 1.1 copy-done.8
  31.8 5.2 %all-to-all-start.1 = ((bf16[32,16,2048]{2,1,0:T(8,128)(2,1)}), bf16[32,16,2048]{2,1,0:T(8,128)(2,1)S(1)}, u32[]{:S(2)}, u32[]{:S(2)}) async-start(bf16[32,16,2048]{2,1,0:T(8,128)(2,1)} %bitcast.18), calls=%async_computation.1 | async-start | bytes 4194304 | tf_op jit(solution)/shard_map/all_to_all | solution.py:322
  37.0 0.0 copy-start.9
  37.0 0.0 copy-start.10
  37.0 2.0 %pack.3 = bf16[4,8,2,8,768]{4,3,2,1,0:T(8,128)(2,1)} custom-call(bf16[2,4,2,8,8,2048]{5,4,3,2,1,0:T(8,128)(2,1)} %bitcast.17), custom_call_target="tpu_custom_call" | custom-call | tf_op jit(solution)/shard_map/pack/pallas_call | solution.py:78
  39.0 7.0 %collective-permute-start = (bf16[32,16,768]{2,1,0:T(8,128)(2,1)}, bf16[32,16,768]{2,1,0:T(8,128)(2,1)}, u32[]{:S(2)}, u32[]{:S(2)}) collective-permute-start(bf16[32,16,768]{2,1,0:T(8,128)(2,1)} %bitcast.22), channel_id=1, source_target_pairs={{0,32},{32,0},{1,33},{33,1},{2,34},{34,2},{3,35},{35,3},{4,36},{36... | collective-permute-start | bytes 2359304 | tf_op jit(solution)/shard_map/ppermute | solution.py:336
  46.0 0.1 subtract_select_fusion
  46.1 0.2 fusion.15
  46.3 4.0 %multiply_convert_fusion.1 = (bf16[1,7,32,512]{3,2,1,0:T(8,128)(2,1)S(1)}, bf16[1,7,32,512]{3,2,1,0:T(8,128)(2,1)S(1)}, bf16[1,7,32,512]{3,2,1,0:T(8,128)(2,1)S(1)}, bf16[1,7,32,512]{3,2,1,0:T(8,128)(2,1)S(1)}) fusion(f32[7,512]{1,0:T(8,128)S(1)} %get-tuple-element.34, s32[7,512]{1,0:T(8,128)S(1)} %get-tuple-element.42, s32[32]{0:T(128)S(1)} %copy-done.10, ...), kind=kLoop, calls=%fused_computation.19 | loop fusion | flops 4587520 | bytes 1003648 | tf_op jit(solution)/shard_map/convert.1
  50.3 2.1 %slice.9 = bf16[32,16,768]{2,1,0:T(8,128)(2,1)} slice(bf16[32,16,1280]{2,1,0:T(8,128)(2,1)} %copy-done.8), slice={[0:32], [0:16], [0:768]} | slice | bytes 1572864 | tf_op jit(solution)/shard_map/slice | solution.py:339
  52.4 0.0 collective-permute-start.2
  52.5 14.8 %collective-permute-done = bf16[32,16,768]{2,1,0:T(8,128)(2,1)} collective-permute-done((bf16[32,16,768]{2,1,0:T(8,128)(2,1)}, bf16[32,16,768]{2,1,0:T(8,128)(2,1)}, u32[]{:S(2)}, u32[]{:S(2)}) %collective-permute-start) | collective-permute-done | bytes 786464 | tf_op jit(solution)/shard_map/ppermute | solution.py:336
  67.2 10.1 %all-to-all-start.2 = ((bf16[32,16,768]{2,1,0:T(8,128)(2,1)}), bf16[32,16,768]{2,1,0:T(8,128)(2,1)}, u32[]{:S(2)}, u32[]{:S(2)}) async-start(bf16[32,16,768]{2,1,0:T(8,128)(2,1)} %collective-permute-done), calls=%async_computation.2 | async-start | bytes 1572864 | tf_op jit(solution)/shard_map/all_to_all | solution.py:322
  77.3 1.9 %slice.8 = bf16[32,16,512]{2,1,0:T(8,128)(2,1)} slice(bf16[32,16,1280]{2,1,0:T(8,128)(2,1)} %copy-done.8), slice={[0:32], [0:16], [768:1280]} | slice | bytes 1048576 | tf_op jit(solution)/shard_map/slice | solution.py:340
  79.2 5.8 %collective-permute-start.1 = (bf16[32,16,512]{2,1,0:T(8,128)(2,1)}, bf16[32,16,512]{2,1,0:T(8,128)(2,1)S(1)}, u32[]{:S(2)}, u32[]{:S(2)}) collective-permute-start(bf16[32,16,512]{2,1,0:T(8,128)(2,1)} %slice.8), channel_id=1, source_target_pairs={{0,32},{32,0},{1,33},{33,1},{2,34},{34,2},{3,35},{35,3},{4,36},{36... | collective-permute-start | bytes 1572872 | tf_op jit(solution)/shard_map/ppermute | solution.py:340
  85.0 0.8 partial.1
  85.8 0.9 copy-done
  86.7 4.7 %collective-permute-done.2.x_ref = bf16[32,16,768]{2,1,0:T(8,128)(2,1)} collective-permute-done((bf16[32,16,768]{2,1,0:T(8,128)(2,1)}, bf16[32,16,768]{2,1,0:T(8,128)(2,1)}, u32[]{:S(2)}, u32[]{:S(2)}) %collective-permute-start.2) | collective-permute-done | bytes 786464 | tf_op jit(solution)/shard_map/ppermute | solution.py:339
  91.4 2.6 %middle.1 = (bf16[448,2048]{1,0:T(8,128)(2,1)}, f32[448,224]{1,0:T(8,128)S(1)}, bf16[448,768]{1,0:T(8,128)(2,1)S(1)}) custom-call(bf16[448,512]{1,0:T(8,128)(2,1)S(1)} %bitcast.10, bf16[32,16,768]{2,1,0:T(8,128)(2,1)} %collective-permute-done.2.x_ref, f32[448,768]{1,0:T(8,128)S(1)} %get-tuple-element.19.p_ref), custom_call_target="tpu_custom_call" | custom-call | flops 352321536 | bytes 4194304 | tf_op jit(solution)/shard_map/middle/pallas_call | solution.py:190
  94.1 0.8 copy-done.2
  94.9 0.8 copy-done.6
  95.7 3.2 %whole.1 = (bf16[448,2048]{1,0:T(8,128)(2,1)}, f32[448,224]{1,0:T(8,128)S(1)}, bf16[448,768]{1,0:T(8,128)(2,1)S(1)}) custom-call(bf16[448,512]{1,0:T(8,128)(2,1)S(1)} %bitcast.14, bf16[448,512]{1,0:T(8,128)(2,1)S(1)} %bitcast.11, bf16[32,16,2048]{2,1,0:T(8,128)(2,1)S(1)} %all-to-all-done.1.x_ref.x0_ref, ...), custom_call_target="tpu_custom_call", output_to_operand_aliasing={{0}: (4, {})} | custom-call | flops 704643072 | bytes 4194304 | tf_op jit(solution)/shard_map/whole/pallas_call | solution.py:127
  98.9 0.8 copy-done.4
  99.8 8.3 %collective-permute-done.1.x_ref = bf16[32,16,512]{2,1,0:T(8,128)(2,1)S(1)} collective-permute-done((bf16[32,16,512]{2,1,0:T(8,128)(2,1)}, bf16[32,16,512]{2,1,0:T(8,128)(2,1)S(1)}, u32[]{:S(2)}, u32[]{:S(2)}) %collective-permute-start.1) | collective-permute-done | bytes 524320 | tf_op jit(solution)/shard_map/ppermute | solution.py:340
  108.1 1.3 rest.1
  109.3 13.1 %all_to_all.25 = bf16[16,8,256]{2,1,0:T(8,128)(2,1)S(1)} all-to-all(bf16[16,8,256]{2,1,0:T(8,128)(2,1)S(1)} %get-tuple-element.26), channel_id=1, replica_groups=mesh['y'=4,'zh'=2,'x'=4,'c'=2,'zl'=4] {'y','x'}, dimensions={0} | all-to-all | bytes 131072 | tf_op jit(solution)/shard_map/all_to_all | solution.py:322
  122.4 45.5 %all_to_all.26.t_ref = bf16[16,8,256]{2,1,0:T(8,128)(2,1)S(1)} all-to-all(bf16[16,8,256]{2,1,0:T(8,128)(2,1)S(1)} %broadcast_in_dim.11), channel_id=1, replica_groups=mesh['y'=4,'zh'=2,'x'=4,'c'=2,'zl'=4] {'zh','zl','c'}, dimensions={0} | all-to-all | bytes 131072 | tf_op jit(solution)/shard_map/all_to_all | solution.py:318
  167.9 2.8 %power.1 = f32[448,2048]{1,0:T(8,128)} custom-call(bf16[16,8,256]{2,1,0:T(8,128)(2,1)S(1)} %all_to_all.26.t_ref, bf16[448,768]{1,0:T(8,128)(2,1)S(1)} %copy-done.3, bf16[448,512]{1,0:T(8,128)(2,1)S(1)} %get-tuple-element.28.refs_1_, bf16[448,768]{1,0:T(8,128)(2,1)S(1)} %copy-done.5), custom_call_target="tpu_custom_call" | custom-call | tf_op jit(solution)/shard_map/power/pallas_call | solution.py:301
  (22 shorter events, 0.2 us)
Async XLA Ops:
  2.9 27.9 %all-to-all-start = ((bf16[32,16,1280]{2,1,0:T(8,128)(2,1)}), bf16[32,16,1280]{2,1,0:T(8,128)(2,1)S(1)}, u32[]{:S(2)}, u32[]{:S(2)}) async-start(bf16[32,16,1280]{2,1,0:T(8,128)(2,1)} %bitcast.20), calls=%async_computation | async-start | bytes 2621440 | tf_op jit(solution)/shard_map/all_to_all | solution.py:322
  30.7 1.1 copy-start.8
  31.8 35.4 %all-to-all-start.1 = ((bf16[32,16,2048]{2,1,0:T(8,128)(2,1)}), bf16[32,16,2048]{2,1,0:T(8,128)(2,1)S(1)}, u32[]{:S(2)}, u32[]{:S(2)}) async-start(bf16[32,16,2048]{2,1,0:T(8,128)(2,1)} %bitcast.18), calls=%async_computation.1 | async-start | bytes 4194304 | tf_op jit(solution)/shard_map/all_to_all | solution.py:322
  37.0 9.0 %copy-start.9 = (s32[7]{0:T(128)S(1)}, s32[7]{0:T(128)}, u32[]{:S(2)}) copy-start(s32[7]{0:T(128)} %param.4) | copy-start | bytes 88
  37.0 9.3 %copy-start.10 = (s32[32]{0:T(128)S(1)}, s32[32]{0:T(128)}, u32[]{:S(2)}) copy-start(s32[32]{0:T(128)} %param.5) | copy-start | bytes 388
  39.0 28.2 %collective-permute-start = (bf16[32,16,768]{2,1,0:T(8,128)(2,1)}, bf16[32,16,768]{2,1,0:T(8,128)(2,1)}, u32[]{:S(2)}, u32[]{:S(2)}) collective-permute-start(bf16[32,16,768]{2,1,0:T(8,128)(2,1)} %bitcast.22), channel_id=1, source_target_pairs={{0,32},{32,0},{1,33},{33,1},{2,34},{34,2},{3,35},{35,3},{4,36},{36... | collective-permute-start | bytes 2359304 | tf_op jit(solution)/shard_map/ppermute | solution.py:336
  52.4 39.0 %collective-permute-start.2 = (bf16[32,16,768]{2,1,0:T(8,128)(2,1)}, bf16[32,16,768]{2,1,0:T(8,128)(2,1)}, u32[]{:S(2)}, u32[]{:S(2)}) collective-permute-start(bf16[32,16,768]{2,1,0:T(8,128)(2,1)} %slice.9), channel_id=1, source_target_pairs={{0,32},{32,0},{1,33},{33,1},{2,34},{34,2},{3,35},{35,3},{4,36},{36... | collective-permute-start | bytes 2359304 | tf_op jit(solution)/shard_map/ppermute | solution.py:339
  67.2 28.4 %all-to-all-start.2 = ((bf16[32,16,768]{2,1,0:T(8,128)(2,1)}), bf16[32,16,768]{2,1,0:T(8,128)(2,1)}, u32[]{:S(2)}, u32[]{:S(2)}) async-start(bf16[32,16,768]{2,1,0:T(8,128)(2,1)} %collective-permute-done), calls=%async_computation.2 | async-start | bytes 1572864 | tf_op jit(solution)/shard_map/all_to_all | solution.py:322
  79.2 28.9 %collective-permute-start.1 = (bf16[32,16,512]{2,1,0:T(8,128)(2,1)}, bf16[32,16,512]{2,1,0:T(8,128)(2,1)S(1)}, u32[]{:S(2)}, u32[]{:S(2)}) collective-permute-start(bf16[32,16,512]{2,1,0:T(8,128)(2,1)} %slice.8), channel_id=1, source_target_pairs={{0,32},{32,0},{1,33},{33,1},{2,34},{34,2},{3,35},{35,3},{4,36},{36... | collective-permute-start | bytes 1572872 | tf_op jit(solution)/shard_map/ppermute | solution.py:340
  85.8 0.9 copy-start
  94.0 0.8 copy-start.2
  94.9 0.8 copy-start.6
  95.7 12.4 %copy-start.1 = (f32[448,512]{1,0:T(8,128)S(1)}, f32[448,512]{1,0:T(8,128)}, u32[]{:S(2)}) copy-start(f32[448,512]{1,0:T(8,128)} %copy-done) | copy-start | bytes 2752516
  95.7 12.4 %copy-start.7 = (f32[448,224]{1,0:T(8,128)S(1)}, f32[448,224]{1,0:T(8,128)}, u32[]{:S(2)}) copy-start(f32[448,224]{1,0:T(8,128)} %copy-done.6) | copy-start | bytes 1204228
  98.9 0.9 copy-start.4
  108.0 59.8 %copy-start.3 = (bf16[448,768]{1,0:T(8,128)(2,1)S(1)}, bf16[448,768]{1,0:T(8,128)(2,1)}, u32[]{:S(2)}) copy-start(bf16[448,768]{1,0:T(8,128)(2,1)} %copy-done.2) | copy-start | bytes 2064388
  108.0 59.8 %copy-start.5 = (bf16[448,768]{1,0:T(8,128)(2,1)S(1)}, bf16[448,768]{1,0:T(8,128)(2,1)}, u32[]{:S(2)}) copy-start(bf16[448,768]{1,0:T(8,128)(2,1)} %copy-done.4) | copy-start | bytes 2064388
